TPU v7x, 256 devices: a whole 4x4x8 slice. The times are simulated.
256 devices in a mesh: seq: 128 (over y, x_hi, z, core), fsdp: 2 (over x_lo).
Axes of the slice: x: 4 (x_hi: 2, x_lo: 2; x = x_hi * 2 + x_lo), y: 4, z: 8, core: 2. Of those that a mesh axis runs over, the one named last changes fastest.
Arguments:
- tokens: bfloat16 [512, 8192], P('seq', 'fsdp'), may hold values from -6 to 6
- gate_weight: bfloat16 [8192, 16384], P('fsdp', 'seq'), may hold values from -0.0625 to 0.0625
- up_weight: bfloat16 [8192, 16384], P('fsdp', 'seq'), may hold values from -0.0625 to 0.0625
- down_weight: bfloat16 [8192, 16384], P('fsdp', 'seq'), may hold values from -0.046875 to 0.046875
Outputs:
- mixed_out: bfloat16 [512, 8192], P('seq', 'fsdp')
All inputs are finite; a program needn't handle non-finite values.
Results may differ from a plain program's by a relative error of at most 0.0049.
Values may be sent and summed in bfloat16 or wider, within the bound.
No kernel may reach another device: no remote copies, remote signals or barrier semaphores. Data moves between devices by JAX's collectives and lax.ppermute only.
A program may use at most 64 MiB of HBM per device.

v0:
```python
import jax
import jax.numpy as jnp
from jax import lax
from jax.sharding import Mesh
from jax.sharding import PartitionSpec as P

SEQ = ("seq_0", "seq_1", "seq_2", "seq_3")


def sent_to_all(value, axis):
    copies = jnp.broadcast_to(value, (lax.axis_size(axis), *value.shape))
    return lax.all_to_all(copies, axis, split_axis=0, concat_axis=0, tiled=True)


def laid_out(pieces, dim):
    dims = list(pieces.shape[1:])
    dims[dim] *= pieces.shape[0]
    return jnp.moveaxis(pieces, 0, dim).reshape(dims)


def gathered_by_axis(value, axes, dim):
    far, near = axes
    first = sent_to_all(value, far)
    pieces = jnp.swapaxes(sent_to_all(first, near), 0, 1)
    return laid_out(pieces.reshape(-1, *value.shape), dim)


def taken_together(value, axis):
    return sent_to_all(value, axis).sum(axis=0)


def in_blocks(value, dim, devices):
    dims = value.shape
    pieces = value.reshape(*dims[:dim], devices, dims[dim] // devices, *dims[dim + 1 :])
    return jnp.moveaxis(pieces, dim, 0)


def sent_and_summed(value, axis, dim):
    pieces = in_blocks(value, dim, lax.axis_size(axis))
    arrived = lax.all_to_all(pieces, axis, split_axis=0, concat_axis=0, tiled=True)
    return arrived.sum(axis=0)


def sum_by_axis(value, axes, dim):
    far, near = axes
    own = sent_and_summed(in_blocks(value, dim, lax.axis_size(far)), near, dim + 1)
    return jnp.sum(lax.all_to_all(own, far, 0, 0, tiled=True), axis=0)


def project_down(hidden, weight):
    return lax.dot_general(
        hidden, weight, (((1,), (1,)), ((), ())), preferred_element_type=jnp.float32
    )


def on_device(tokens, gate_weight, up_weight, down_weight):
    units = gate_weight.shape[1]
    paired = jnp.concatenate([gate_weight, up_weight], axis=1)
    parts = jnp.dot(
        gathered_by_axis(tokens, (("seq_0", "seq_1", "seq_2"), "seq_3"), 0),
        paired,
        preferred_element_type=jnp.float32,
    )
    values = taken_together(parts, "fsdp")
    hidden = (jax.nn.silu(values[:, :units]) * values[:, units:]).astype(jnp.bfloat16)
    return sum_by_axis(
        project_down(hidden, down_weight), (("seq_0", "seq_1", "seq_2"), "seq_3"), 0
    ).astype(jnp.bfloat16)


def solution(mesh):
    finer = Mesh(
        mesh.devices.reshape(4, 2, 8, 2, mesh.shape["fsdp"]),
        ("seq_0", "seq_1", "seq_2", "seq_3", "fsdp"),
    )
    in_specs = (P(SEQ, "fsdp"), P("fsdp", SEQ), P("fsdp", SEQ), P("fsdp", SEQ))
    out_specs = P(SEQ, "fsdp")
    return jax.shard_map(
        on_device, mesh=finer, in_specs=in_specs, out_specs=out_specs, check_vma=False
    )
```

profile of v0, /device:TPU:8, one launch (start us, length us, event | category | flops | bytes accessed | tf_op | source)
XLA Modules:
  0.0 268.0 jit_solution(1692284464820322368)
XLA Ops:
  0.0 0.0 copy-start
  0.0 1.8 broadcast_in_dim.9
  1.9 66.5 %all_to_all.25 = bf16[64,4,4096]{2,1,0:T(4,128)(2,1)S(1)} all-to-all(bf16[64,4,4096]{2,1,0:T(4,128)(2,1)S(1)} %broadcast_in_dim.9), channel_id=1, replica_groups=mesh['seq_0'=4,'seq_1'=2,'seq_2'=8,'seq_3'=2,'fsdp'=2] {'seq_0','seq_1',..., dimensions={0} | all-to-all | bytes 4194304 | tf_op jit(solution)/shard_map/all_to_all | solution.py:12
  68.3 2.9 %broadcast_in_dim.10 = bf16[2,64,4,4096]{3,2,1,0:T(4,128)(2,1)S(1)} broadcast(bf16[64,4,4096]{2,1,0:T(4,128)(2,1)S(1)} %all_to_all.25), dimensions={1,2,3} | broadcast | bytes 6291456 | tf_op jit(solution)/shard_map/broadcast_in_dim | solution.py:11
  71.2 7.1 %all_to_all.26 = bf16[2,64,4,4096]{3,2,1,0:T(4,128)(2,1)S(1)} all-to-all(bf16[2,64,4,4096]{3,2,1,0:T(4,128)(2,1)S(1)} %broadcast_in_dim.10), channel_id=1, replica_groups=mesh['seq_0'=4,'seq_1'=2,'seq_2'=8,'seq_3'=2,'fsdp'=2] {'seq_3'}, dimensions={0} | all-to-all | bytes 8388608 | tf_op jit(solution)/shard_map/all_to_all | solution.py:12
  78.3 3.9 %copy.13 = bf16[64,2,4,4096]{3,2,1,0:T(4,128)(2,1)} copy(bf16[64,2,4,4096]{3,2,0,1:T(4,128)(2,1)S(1)} %bitcast.9) | data formatting | bytes 8388608 | tf_op jit(solution)/shard_map/transpose | solution.py:24
  82.2 0.0 copy-start.2
  82.2 7.0 %reshape_reshape.6 = bf16[512,4096]{1,0:T(8,128)(2,1)} reshape(bf16[64,2,4,4096]{3,2,1,0:T(4,128)(2,1)} %copy.13) | data formatting | bytes 8388608 | tf_op jit(solution)/shard_map/reshape;reshape | solution.py:18
  89.2 0.0 copy-done.2
  89.2 3.8 %fusion.4 = f32[512,256]{0,1:T(8,128)S(1)} fusion(bf16[512,4096]{1,0:T(8,128)(2,1)} %reshape_reshape.6, bf16[4096,128]{1,0:T(8,128)(2,1)S(1)} %copy-done.2, bf16[4096,128]{1,0:T(8,128)(2,1)} %param.5), kind=kOutput, calls=%fused_computation.5 | convolution fusion | flops 1077936128 | bytes 6815744 | tf_op jit(solution)/shard_map/dot_general | solution.py:59
  93.0 0.2 copy.14
  93.2 0.1 broadcast_in_dim.11
  93.3 16.6 %all_to_all.27 = f32[2,512,256]{2,1,0:T(8,128)S(1)} all-to-all(f32[2,512,256]{2,1,0:T(8,128)S(1)} %broadcast_in_dim.11), channel_id=1, replica_groups=mesh['seq_0'=4,'seq_1'=2,'seq_2'=8,'seq_3'=2,'fsdp'=2] {'fsdp'}, dimensions={0} | all-to-all | bytes 2097152 | tf_op jit(solution)/shard_map/all_to_all | solution.py:12
  110.0 0.1 reduce_sum.27
  110.1 0.0 copy-done
  110.1 4.5 %fusion.8 = f32[512,4096]{1,0:T(8,128)} fusion(bf16[4096,128]{1,0:T(8,128)(2,1)S(1)} %copy-done, f32[512,256]{1,0:T(8,128)S(1)} %reduce_sum.27), kind=kOutput, calls=%fused_computation.8 | convolution fusion | flops 537264128 | bytes 9961472 | tf_op jit(solution)/shard_map/dot_general | solution.py:51
  114.5 9.8 %reshape_reshape.7 = f32[64,2,4,4096]{3,2,1,0:T(4,128)} reshape(f32[512,4096]{1,0:T(8,128)} %fusion.8) | data formatting | bytes 16777216 | tf_op jit(solution)/shard_map/reshape;reshape | solution.py:34
  124.3 7.7 %copy.19 = f32[64,2,4,4096]{3,2,0,1:T(4,128)} copy(f32[64,2,4,4096]{3,2,1,0:T(4,128)} %reshape_reshape.7) | data formatting | bytes 16777216 | tf_op jit(solution)/shard_map/reshape;reshape | solution.py:34
  132.0 18.5 %all_to_all.28 = f32[2,64,4,4096]{3,2,1,0:T(4,128)} all-to-all(f32[2,64,4,4096]{3,2,1,0:T(4,128)} %bitcast.8), channel_id=1, replica_groups=mesh['seq_0'=4,'seq_1'=2,'seq_2'=8,'seq_3'=2,'fsdp'=2] {'seq_3'}, dimensions={0} | all-to-all | bytes 16777216 | tf_op jit(solution)/shard_map/all_to_all | solution.py:40
  150.5 9.2 %reduce_sum.28 = f32[64,4,4096]{2,1,0:T(4,128)} reduce(f32[2,64,4,4096]{3,2,1,0:T(4,128)} %all_to_all.28, f32[]{:T(128)} %constant.1.clone.1), dimensions={0}, to_apply=%region_1.2 | reduce | flops 1048576 | bytes 12582916 | tf_op jit(solution)/shard_map/reduce_sum | solution.py:41
  159.7 0.0 copy-start.1
  159.7 104.8 %all_to_all.29 = f32[64,4,4096]{2,1,0:T(4,128)} all-to-all(f32[64,4,4096]{2,1,0:T(4,128)} %reduce_sum.28), channel_id=1, replica_groups=mesh['seq_0'=4,'seq_1'=2,'seq_2'=8,'seq_3'=2,'fsdp'=2] {'seq_0','seq_1',..., dimensions={0} | all-to-all | bytes 8388608 | tf_op jit(solution)/shard_map/all_to_all | solution.py:47
  264.5 3.4 %reduce_sum.29 = bf16[4,4096]{1,0:T(4,128)(2,1)} reduce(f32[64,4,4096]{2,1,0:T(4,128)} %all_to_all.29, f32[]{:T(128)} %constant.1.clone.1), dimensions={0}, to_apply=%region_2.3 | reduce | flops 1032192 | bytes 4227076 | tf_op jit(solution)/shard_map/reduce_sum | solution.py:47
  267.9 0.0 copy-done.1
Async XLA Ops:
  0.0 110.1 %copy-start = (bf16[4096,128]{1,0:T(8,128)(2,1)S(1)}, bf16[4096,128]{1,0:T(8,128)(2,1)}, u32[]{:S(2)}) copy-start(bf16[4096,128]{1,0:T(8,128)(2,1)} %param.7) | copy-start | bytes 3145732
  82.2 7.0 %copy-start.2 = (bf16[4096,128]{1,0:T(8,128)(2,1)S(1)}, bf16[4096,128]{1,0:T(8,128)(2,1)}, u32[]{:S(2)}) copy-start(bf16[4096,128]{1,0:T(8,128)(2,1)} %param.6) | copy-start | bytes 3145732
  159.7 108.3 %copy-start.1 = (bf16[4096,128]{1,0:T(8,128)(2,1)S(1)}, bf16[4096,128]{1,0:T(8,128)(2,1)}, u32[]{:S(2)}) copy-start(bf16[4096,128]{1,0:T(8,128)(2,1)} %param.7) | copy-start | bytes 3145732
where the time goes:
time: 269 us; the launch traced here: 268 us
  blocking collectives  214 us (80%)
  local copies, waits for them, and re-layouts  33.4 us (12%)
  other arithmetic  12.7 us (5%)
  matrix products  8.28 us (3%)
    all_to_all x1, blocking collectives, sum_by_axis(): return jnp.sum(lax.all_to_all(own, far, 0, 0, tiled=True), axis=0)  105 us
    all_to_all x3, blocking collectives, sent_to_all(): return lax.all_to_all(copies, axis, split_axis=0, concat_axis=0, tiled=True)  90.2 us
    all_to_all x1, blocking collectives, sent_and_summed(): lax.all_to_all(pieces, axis, split_axis=0, concat_axis=0, tiled=True)  18.5 us
    another operation x2, local copies, waits for them, and re-layouts, in_blocks(): value.reshape(*dims[:dim], devices, dims[dim] // devices, *dims[dim + 1:])  17.5 us
    reduce_sum x1, other arithmetic, sent_and_summed(): return arrived.sum(axis=0)  9.17 us
    another operation x1, local copies, waits for them, and re-layouts, laid_out(): return jnp.moveaxis(pieces, 0, dim).reshape(dims)  6.99 us

commit v1 on v0

v1 whole, which is shorter than its diff:
```python
import jax
import jax.numpy as jnp
from jax import lax
from jax.sharding import Mesh
from jax.sharding import PartitionSpec as P

AXES = ("y", "h", "z", "c")
PLANE = ("y", "h")
F32, BF16 = jnp.float32, jnp.bfloat16


def swapped(value, axis):
    return lax.ppermute(value, axis, [(0, 1), (1, 0)])


def shared(value, axes):
    copies = jnp.broadcast_to(value, (lax.axis_size(axes), *value.shape))
    return lax.all_to_all(copies, axes, 0, 0, tiled=True)


def summed(pieces, axes):
    arrived = lax.all_to_all(pieces, axes, 0, 0, tiled=True)
    return arrived.astype(F32).sum(axis=0)


def on_device(tokens, gate_weight, up_weight, down_weight):
    own, width = tokens.shape
    gates = jnp.concatenate([gate_weight, swapped(gate_weight, "c")], axis=1)
    ups = jnp.concatenate([up_weight, swapped(up_weight, "c")], axis=1)
    downs = jnp.concatenate([down_weight, swapped(down_weight, "c")], axis=1)
    line = shared(tokens, "z").reshape(-1, width)
    rows = shared(line, PLANE).reshape(-1, width)
    units = gates.shape[1]
    parts = jnp.dot(
        rows, jnp.concatenate([gates, ups], axis=1), preferred_element_type=F32
    )
    values = parts + swapped(parts.astype(BF16), "fsdp").astype(F32)
    hidden = (jax.nn.silu(values[:, :units]) * values[:, units:]).astype(BF16)
    out = lax.dot_general(
        hidden, downs, (((1,), (1,)), ((), ())), preferred_element_type=F32
    ).astype(BF16)
    mine = summed(out.reshape(-1, *line.shape), PLANE).astype(BF16)
    return summed(mine.reshape(-1, own, width), "z").astype(BF16)


def solution(mesh):
    finer = Mesh(
        mesh.devices.reshape(4, 2, 8, 2, mesh.shape["fsdp"]), (*AXES, "fsdp")
    )
    in_specs = (P(AXES, "fsdp"), P("fsdp", AXES), P("fsdp", AXES), P("fsdp", AXES))
    out_specs = P(AXES, "fsdp")
    return jax.shard_map(
        on_device, mesh=finer, in_specs=in_specs, out_specs=out_specs, check_vma=False
    )
```

time: 269 us -> 114 us (0.42)
  blocking collectives: 214 us -> 66.4 us
  local copies, waits for them, and re-layouts: 33.4 us -> 3.55 us
  waiting for transfers between devices: 0 us -> 28.3 us
  other arithmetic: 12.7 us -> 1.13 us
  starting transfers between devices: 0 us -> 8.79 us
  matrix products: 8.28 us -> 5.26 us
    all_to_all x5 -> x3, blocking collectives: 214 us -> 66.4 us  [the longest x2 46.3 us: summed(): arrived = lax.all_to_all(pieces, axes, 0, 0, tiled=True)]
    another operation x3 -> x0, local copies, waits for them, and re-layouts: 24.5 us -> none  [the longest x2 17.5 us: in_blocks(): value.reshape(*dims[:dim], devices, dims[dim] // devices, *dims[dim + 1:])]
    all_to_all x0 -> x1, waiting for transfers between devices: none -> 19.6 us  [shared(): return lax.all_to_all(copies, axes, 0, 0, tiled=True)]
    reduce_sum x3 -> x2, other arithmetic: 12.7 us -> 1.07 us  [summed(): return arrived.astype(F32).sum(axis=0)]
    ppermute x0 -> x4, waiting for transfers between devices: none -> 8.69 us  [swapped(): return lax.ppermute(value, axis, [(0, 1), (1, 0)])]
    all_to_all x0 -> x1, starting transfers between devices: none -> 7.51 us  [shared(): return lax.all_to_all(copies, axes, 0, 0, tiled=True)]
    transpose x1 -> x0, local copies, waits for them, and re-layouts: 3.92 us -> none  [gathered_by_axis(): pieces = jnp.swapaxes(sent_to_all(first, near), 0, 1)]
    dot_general x2, matrix products: 8.28 us -> 5.26 us  [the longest x1 3.24 us: on_device(): jnp.dot(rows, jnp.concatenate([gates, ups], axis=1), preferred_element_ty...]
  transfers between devices with their start and end apart: 0 -> 5, of which waited for: 0 -> 4; matrix products, arithmetic and copies ran while one was open for 0% -> 3% of each run, Pallas kernels for 0% -> 0%
where the time goes in v1:
time: 114 us
  blocking collectives  66.4 us (58%)
  waiting for transfers between devices  28.3 us (25%)
  starting transfers between devices  8.79 us (8%)
  matrix products  5.26 us (5%)
  local copies, waits for them, and re-layouts  3.55 us (3%)
    all_to_all x2, blocking collectives, summed(): arrived = lax.all_to_all(pieces, axes, 0, 0, tiled=True)  46.3 us
    all_to_all x1, blocking collectives, shared(): return lax.all_to_all(copies, axes, 0, 0, tiled=True)  20.1 us
    all_to_all x1, waiting for transfers between devices, shared(): return lax.all_to_all(copies, axes, 0, 0, tiled=True)  19.6 us
    ppermute x4, waiting for transfers between devices, swapped(): return lax.ppermute(value, axis, [(0, 1), (1, 0)])  8.69 us
    all_to_all x1, starting transfers between devices, shared(): return lax.all_to_all(copies, axes, 0, 0, tiled=True)  7.51 us
    dot_general x1, matrix products, on_device(): jnp.dot(rows, jnp.concatenate([gates, ups], axis=1), preferred_element_ty...  3.24 us
    broadcast_in_dim x2, local copies, waits for them, and re-layouts, shared(): copies = jnp.broadcast_to(value, (lax.axis_size(axes), *value.shape))  2.4 us
  transfers between devices with their start and end apart: 5, of which 4 were waited for; matrix products, arithmetic and copies ran while one was open for 3% of the time, Pallas kernels for 0%

profile of v1, /device:TPU:8, one launch (start us, length us, event | category | flops | bytes accessed | tf_op | source)
XLA Modules:
  0.0 113.5 jit_solution(7926791969034123362)
XLA Ops:
  0.0 0.8 broadcast_in_dim.6
  0.8 20.1 %all_to_all.20 = bf16[8,4,4096]{2,1,0:T(4,128)(2,1)S(1)} all-to-all(bf16[8,4,4096]{2,1,0:T(4,128)(2,1)S(1)} %broadcast_in_dim.6), channel_id=1, replica_groups=mesh['y'=4,'h'=2,'z'=8,'c'=2,'fsdp'=2] {'z'}, dimensions={0} | all-to-all | bytes 524288 | tf_op jit(solution)/shard_map/all_to_all | solution.py:18
  21.0 0.1 reshape.12
  21.0 1.6 %broadcast_in_dim.7 = bf16[8,32,4096]{2,1,0:T(8,128)(2,1)} broadcast(bf16[32,4096]{1,0:T(8,128)(2,1)S(1)} %reshape.12), dimensions={1,2} | broadcast | bytes 2359296 | tf_op jit(solution)/shard_map/broadcast_in_dim | solution.py:17
  22.6 7.5 %all-to-all-start.1 = ((bf16[8,32,4096]{2,1,0:T(8,128)(2,1)}), bf16[8,32,4096]{2,1,0:T(8,128)(2,1)S(1)}, u32[]{:S(2)}, u32[]{:S(2)}) async-start(bf16[8,32,4096]{2,1,0:T(8,128)(2,1)} %broadcast_in_dim.7), calls=%async_computation.1 | async-start | bytes 4194304 | tf_op jit(solution)/shard_map/all_to_all | solution.py:18
  30.1 0.0 collective-permute-start
  30.1 0.0 copy-done
  30.1 0.5 collective-permute-start.1
  30.6 0.1 collective-permute-start.3
  30.7 2.3 %collective-permute-done = bf16[4096,128]{1,0:T(8,128)(2,1)S(1)} collective-permute-done((bf16[4096,128]{1,0:T(8,128)(2,1)}, bf16[4096,128]{1,0:T(8,128)(2,1)S(1)}, u32[]{:S(2)}, u32[]{:S(2)}) %collective-permute-start) | collective-permute-done | bytes 1048608 | tf_op jit(solution)/shard_map/ppermute | solution.py:13
  33.0 1.0 copy-done.2
  34.0 0.6 collective-permute-done.1
  34.6 19.6 %all-to-all-done.1 = bf16[8,32,4096]{2,1,0:T(8,128)(2,1)S(1)} async-done(((bf16[8,32,4096]{2,1,0:T(8,128)(2,1)}), bf16[8,32,4096]{2,1,0:T(8,128)(2,1)S(1)}, u32[]{:S(2)}, u32[]{:S(2)}) %all-to-all-start.1) | async-done | bytes 2097184 | tf_op jit(solution)/shard_map/all_to_all | solution.py:18
  54.2 3.2 %fusion.20 = (bf16[256,512]{0,1:T(8,128)(2,1)S(1)}, f32[256,512]{0,1:T(8,128)S(1)}) fusion(bf16[256,4096]{1,0:T(8,128)(2,1)S(1)} %bitcast.5, bf16[4096,128]{1,0:T(8,128)(2,1)} %collective-permute-done.1, bf16[4096,128]{1,0:T(8,128)(2,1)S(1)} %copy-done, bf16[4096,128]{1,0:T(8,128)(2,1)} %copy-done.2, bf16[4096,128]{1,0:T(8,128)(2,1)} %param.5), kind=kOutput, calls=%fused_computation.20 | convolution fusion | flops 1090650112 | bytes 7077888 | tf_op jit(solution)/shard_map/dot_general | solution.py:34
  57.5 0.7 collective-permute-start.2
  58.1 5.8 %collective-permute-done.2 = bf16[256,512]{0,1:T(8,128)(2,1)S(1)} collective-permute-done((bf16[256,512]{0,1:T(8,128)(2,1)S(1)}, bf16[256,512]{0,1:T(8,128)(2,1)S(1)}, u32[]{:S(2)}, u32[]{:S(2)}) %collective-permute-start.2) | collective-permute-done | bytes 262176 | tf_op jit(solution)/shard_map/ppermute | solution.py:13
  63.9 0.1 convert_add_fusion
  64.0 0.0 collective-permute-done.3
  64.0 2.0 %convolution_convert_fusion = bf16[256,4096]{1,0:T(8,128)(2,1)S(1)} fusion(bf16[4096,128]{1,0:T(8,128)(2,1)} %collective-permute-done.3, bf16[4096,128]{1,0:T(8,128)(2,1)S(1)} %copy-done.1, f32[256,512]{0,1:T(8,128)S(1)} %convert_add_fusion), kind=kOutput, calls=%fused_computation | convolution fusion | flops 542507008 | bytes 4718592 | tf_op jit(solution)/shard_map/dot_general | solution.py:39
  66.0 32.7 %all_to_all.21 = bf16[8,32,4096]{2,1,0:T(8,128)(2,1)S(1)} all-to-all(bf16[8,32,4096]{2,1,0:T(8,128)(2,1)S(1)} %bitcast.6), channel_id=1, replica_groups=mesh['y'=4,'h'=2,'z'=8,'c'=2,'fsdp'=2] {'y','h'}, dimensions={0} | all-to-all | bytes 4194304 | tf_op jit(solution)/shard_map/all_to_all | solution.py:22
  98.7 0.3 reduce_sum.24
  99.1 0.1 reshape.15
  99.2 13.6 %all_to_all.22 = bf16[8,4,4096]{2,1,0:T(4,128)(2,1)S(1)} all-to-all(bf16[8,4,4096]{2,1,0:T(4,128)(2,1)S(1)} %reshape.15), channel_id=1, replica_groups=mesh['y'=4,'h'=2,'z'=8,'c'=2,'fsdp'=2] {'z'}, dimensions={0} | all-to-all | bytes 524288 | tf_op jit(solution)/shard_map/all_to_all | solution.py:22
  112.8 0.7 reduce_sum.25
  (4 shorter events, 0.0 us)
Async XLA Ops:
  22.6 7.5 %copy-start = (bf16[4096,128]{1,0:T(8,128)(2,1)S(1)}, bf16[4096,128]{1,0:T(8,128)(2,1)}, u32[]{:S(2)}) copy-start(bf16[4096,128]{1,0:T(8,128)(2,1)} %param.6) | copy-start | bytes 3145732
  22.6 31.6 %all-to-all-start.1 = ((bf16[8,32,4096]{2,1,0:T(8,128)(2,1)}), bf16[8,32,4096]{2,1,0:T(8,128)(2,1)S(1)}, u32[]{:S(2)}, u32[]{:S(2)}) async-start(bf16[8,32,4096]{2,1,0:T(8,128)(2,1)} %broadcast_in_dim.7), calls=%async_computation.1 | async-start | bytes 4194304 | tf_op jit(solution)/shard_map/all_to_all | solution.py:18
  30.1 2.9 %collective-permute-start = (bf16[4096,128]{1,0:T(8,128)(2,1)}, bf16[4096,128]{1,0:T(8,128)(2,1)S(1)}, u32[]{:S(2)}, u32[]{:S(2)}) collective-permute-start(bf16[4096,128]{1,0:T(8,128)(2,1)} %param.5), channel_id=1, source_target_pairs={{0,2},{2,0},{1,3},{3,1},{4,6},{6,4},{5,7},{7,5},{8,10},{10,8},{9,1... | collective-permute-start | bytes 3145736 | tf_op jit(solution)/shard_map/ppermute | solution.py:13
  30.1 4.5 %collective-permute-start.1 = (bf16[4096,128]{1,0:T(8,128)(2,1)S(1)}, bf16[4096,128]{1,0:T(8,128)(2,1)}, u32[]{:S(2)}, u32[]{:S(2)}) collective-permute-start(bf16[4096,128]{1,0:T(8,128)(2,1)S(1)} %copy-done), channel_id=1, source_target_pairs={{0,2},{2,0},{1,3},{3,1},{4,6},{6,4},{5,7},{7,5},{8,10},{10,8},{9,1... | collective-permute-start | bytes 3145736 | tf_op jit(solution)/shard_map/ppermute | solution.py:13
  30.6 33.4 %collective-permute-start.3 = (bf16[4096,128]{1,0:T(8,128)(2,1)}, bf16[4096,128]{1,0:T(8,128)(2,1)}, u32[]{:S(2)}, u32[]{:S(2)}) collective-permute-start(bf16[4096,128]{1,0:T(8,128)(2,1)} %param.7), channel_id=1, source_target_pairs={{0,2},{2,0},{1,3},{3,1},{4,6},{6,4},{5,7},{7,5},{8,10},{10,8},{9,1... | collective-permute-start | bytes 3145736 | tf_op jit(solution)/shard_map/ppermute | solution.py:13
  33.0 1.0 copy-start.2
  54.2 9.8 %copy-start.1 = (bf16[4096,128]{1,0:T(8,128)(2,1)S(1)}, bf16[4096,128]{1,0:T(8,128)(2,1)}, u32[]{:S(2)}) copy-start(bf16[4096,128]{1,0:T(8,128)(2,1)} %param.7) | copy-start | bytes 3145732
  57.5 6.5 %collective-permute-start.2 = (bf16[256,512]{0,1:T(8,128)(2,1)S(1)}, bf16[256,512]{0,1:T(8,128)(2,1)S(1)}, u32[]{:S(2)}, u32[]{:S(2)}) collective-permute-start(bf16[256,512]{0,1:T(8,128)(2,1)S(1)} %get-tuple-element.5), channel_id=1, source_target_pairs={{0,1},{1,0},{2,3},{3,2},{4,5},{5,4},{6,7},{7,6},{8,9},{9,8},{10,11... | collective-permute-start | bytes 786440 | tf_op jit(solution)/shard_map/ppermute | solution.py:13

commit v2 on v1

v2 whole, which is shorter than its diff:
```python
import jax
import jax.numpy as jnp
from jax import lax
from jax.experimental import pallas as pl
from jax.experimental.pallas import tpu as pltpu
from jax.sharding import Mesh
from jax.sharding import PartitionSpec as P


AXES = ("y", "h", "z", "c")
F32, BF16 = jnp.float32, jnp.bfloat16
STEP = 512
VMEM_LIMIT = 16 * 2**20


def moved(value, axis, step):
    n = lax.axis_size(axis)
    return lax.ppermute(value, axis, [(i, (i + step) % n) for i in range(n)])


def shared(value, axis):
    copies = jnp.broadcast_to(value, (lax.axis_size(axis), *value.shape))
    return lax.all_to_all(copies, axis, 0, 0, tiled=True)


def gathered_in_plane(own):
    before = moved(own, "y", 1)
    after = moved(own, "y", 3)
    other = moved(own, "h", 1)
    far = [moved(halves(before)[0], "y", 1), moved(halves(after)[1], "y", 3)]
    far = jnp.concatenate(far, axis=0)
    b_other = moved(other, "y", 1)
    a_other = moved(other, "y", 3)
    far_other = moved(far, "h", 1)
    return (own, before, after, other), (far, b_other, a_other, far_other)


def plus(first, *others):
    total = first.astype(F32)
    for other in others:
        total = total + other.astype(F32)
    return total.astype(BF16)


def halves(value):
    half = value.shape[0] // 2
    return value[:half], value[half:]


def on_core(kernel, outs, flops, *args):
    vmem = pl.BlockSpec(memory_space=pltpu.VMEM)
    moved_bytes = sum(a.size * a.dtype.itemsize for a in (*args, *outs))
    return pl.pallas_call(
        kernel,
        out_shape=outs,
        in_specs=[vmem] * len(args),
        out_specs=[vmem] * len(outs),
        compiler_params=pltpu.CompilerParams(vmem_limit_bytes=VMEM_LIMIT),
        cost_estimate=pl.CostEstimate(
            flops=flops, transcendentals=0, bytes_accessed=moved_bytes
        ),
    )(*args)


def parts_of(blocks, gates, ups):
    depth, half = gates[0].shape
    rows = sum(b.shape[0] for b in blocks)

    def kernel(*refs):
        *block_refs, g0, g1, u0, u1, out = refs
        for pair, at in (((g0, g1), 0), ((u0, u1), 2 * half)):
            total = jnp.zeros((rows, 2 * half), F32)
            for k in range(0, depth, STEP):
                cut = (slice(None), pl.ds(k, STEP))
                left = jnp.concatenate([b[cut] for b in block_refs], axis=0)
                cut = (pl.ds(k, STEP), slice(None))
                right = jnp.concatenate([w[cut] for w in pair], axis=1)
                total += jnp.dot(left, right, preferred_element_type=F32)
            out[:, at : at + 2 * half] = total

    outs = [jax.ShapeDtypeStruct((rows, 4 * half), F32)]
    flops = 8 * rows * depth * half
    return on_core(kernel, outs, flops, *blocks, *gates, *ups)[0]


def projected(parts, came, downs, sizes):
    width, half = downs[0].shape

    def kernel(parts, came, d0, d1, *outs):
        values = parts[...] + came[...].astype(F32)
        gate, up = values[:, : 2 * half], values[:, 2 * half :]
        hidden = (gate / (1 + jnp.exp(-gate)) * up).astype(BF16)
        for n in range(0, width, STEP):
            cut = (pl.ds(n, STEP), slice(None))
            right = jnp.concatenate([d0[cut], d1[cut]], axis=1)
            out = lax.dot_general(
                hidden, right, (((1,), (1,)), ((), ())), preferred_element_type=F32
            ).astype(BF16)
            at = 0
            for size, ref in zip(sizes, outs):
                ref[:, n : n + STEP] = out[at : at + size]
                at += size

    outs = [jax.ShapeDtypeStruct((size, width), BF16) for size in sizes]
    flops = 4 * sum(sizes) * width * half
    return on_core(kernel, outs, flops, parts, came, *downs)


def summed_in_plane(near, away):
    own, before, after, other = near
    far, b_other, a_other, far_other = away
    far = plus(far, moved(far_other, "h", 1))
    from_after_o = moved(b_other, "y", 3)
    from_before_o = moved(a_other, "y", 1)
    top, bottom = halves(far)
    top = moved(top, "y", 3)
    bottom = moved(bottom, "y", 1)
    before_top, before_bottom = halves(before)
    after_top, after_bottom = halves(after)
    early_top = moved(after_top, "y", 1)
    early_bottom = moved(before_bottom, "y", 3)
    from_other = moved(plus(other, from_after_o, from_before_o), "h", 1)
    late_top = moved(plus(before_top, top), "y", 3)
    late_bottom = moved(plus(after_bottom, bottom), "y", 1)
    early = jnp.concatenate([early_top, early_bottom], axis=0)
    late = jnp.concatenate([late_top, late_bottom], axis=0)
    return plus(own, early, late, from_other)


def on_device(tokens, gate_weight, up_weight, down_weight):
    count, width = tokens.shape
    gates = gate_weight, moved(gate_weight, "c", 1)
    ups = up_weight, moved(up_weight, "c", 1)
    downs = down_weight, moved(down_weight, "c", 1)
    own = shared(tokens, "z").reshape(-1, width)
    near, away = gathered_in_plane(own)
    near = parts_of(near, gates, ups)
    away = parts_of(away, gates, ups)
    near_in = moved(near, "fsdp", 1)
    away_in = moved(away.astype(BF16), "fsdp", 1)
    sizes = (own.shape[0],) * 4
    away = projected(away, away_in, downs, sizes)
    near = projected(near, near_in, downs, sizes)
    mine = summed_in_plane(near, away)
    pieces = mine.reshape(-1, count, width)
    arrived = lax.all_to_all(pieces, "z", 0, 0, tiled=True)
    return plus(*arrived)


def solution(mesh):
    finer = Mesh(
        mesh.devices.reshape(4, 2, 8, 2, mesh.shape["fsdp"]), (*AXES, "fsdp")
    )
    in_specs = (P(AXES, "fsdp"), P("fsdp", AXES), P("fsdp", AXES), P("fsdp", AXES))
    out_specs = P(AXES, "fsdp")

    return jax.shard_map(
        on_device, mesh=finer, in_specs=in_specs, out_specs=out_specs, check_vma=False
    )
```

time: 114 us -> 101 us (0.89); the launches traced: 114 us -> 99 us
  blocking collectives: 66.4 us -> 34 us
  starting transfers between devices: 8.79 us -> 33.1 us
  matrix products: 5.26 us -> 0 us
  waiting for transfers between devices: 28.3 us -> 25.2 us
  Pallas kernels: 0 us -> 3.03 us
  local copies, waits for them, and re-layouts: 3.55 us -> 2.4 us
    all_to_all x3 -> x2, blocking collectives: 66.4 us -> 34 us  [the longest x1 20.3 us: shared(): return lax.all_to_all(copies, axis, 0, 0, tiled=True)]
    ppermute x4 -> x23, starting transfers between devices: 1.28 us -> 33.1 us  [moved(): return lax.ppermute(value, axis, [(i, (i + step) % n) for i in range(n)])]
    all_to_all x1 -> x0, waiting for transfers between devices: 19.6 us -> none  [shared(): return lax.all_to_all(copies, axes, 0, 0, tiled=True)]
    ppermute x4 -> x23, waiting for transfers between devices: 8.69 us -> 25.2 us  [moved(): return lax.ppermute(value, axis, [(i, (i + step) % n) for i in range(n)])]
    all_to_all x1 -> x0, starting transfers between devices: 7.51 us -> none  [shared(): return lax.all_to_all(copies, axes, 0, 0, tiled=True)]
    dot_general x2 -> x0, matrix products: 5.26 us -> none  [the longest x1 3.24 us: on_device(): jnp.dot(rows, jnp.concatenate([gates, ups], axis=1), preferred_element_ty...]
    pallas_call x0 -> x4, Pallas kernels: none -> 3.03 us  [on_core(): pl.pallas_call(kernel, out_shape=outs, in_specs=[vmem] * len(args), out_s...]
    broadcast_in_dim x2 -> x1, local copies, waits for them, and re-layouts: 2.4 us -> 0.92 us  [shared(): copies = jnp.broadcast_to(value, (lax.axis_size(axis), *value.shape))]
  transfers between devices with their start and end apart: 5 -> 23, of which waited for: 4 -> 12; matrix products, arithmetic and copies ran while one was open for 3% -> 0% of each run, Pallas kernels for 0% -> 3%
where the time goes in v2:
time: 101 us; the launch traced here: 99 us
  blocking collectives  34 us (34%)
  starting transfers between devices  33.1 us (33%)
  waiting for transfers between devices  25.2 us (25%)
  Pallas kernels  3.03 us (3%)
  local copies, waits for them, and re-layouts  2.4 us (2%)
  other arithmetic  1.07 us (1%)
    ppermute x23, starting transfers between devices, moved(): return lax.ppermute(value, axis, [(i, (i + step) % n) for i in range(n)])  33.1 us
    ppermute x23, waiting for transfers between devices, moved(): return lax.ppermute(value, axis, [(i, (i + step) % n) for i in range(n)])  25.2 us
    all_to_all x1, blocking collectives, shared(): return lax.all_to_all(copies, axis, 0, 0, tiled=True)  20.3 us
    all_to_all x1, blocking collectives, on_device(): arrived = lax.all_to_all(pieces, 'z', 0, 0, tiled=True)  13.7 us
    pallas_call x4, Pallas kernels, on_core(): pl.pallas_call(kernel, out_shape=outs, in_specs=[vmem] * len(args), out_s...  3.03 us
  transfers between devices with their start and end apart: 23, of which 12 were waited for; matrix products, arithmetic and copies ran while one was open for 0% of the time, Pallas kernels for 3%

profile of v2, /device:TPU:8, one launch (start us, length us, event | category | flops | bytes accessed | tf_op | source)
XLA Modules:
  0.0 99.0 jit_solution(11082164334309757299)
XLA Ops:
  0.9 20.3 %all_to_all.10 = bf16[8,4,4096]{2,1,0:T(4,128)(2,1)S(1)} all-to-all(bf16[8,4,4096]{2,1,0:T(4,128)(2,1)S(1)} %broadcast_in_dim.3), channel_id=1, replica_groups=mesh['y'=4,'h'=2,'z'=8,'c'=2,'fsdp'=2] {'z'}, dimensions={0} | all-to-all | bytes 524288 | tf_op jit(solution)/shard_map/all_to_all | solution.py:23
  21.3 1.7 %collective-permute-start = (bf16[32,4096]{1,0:T(8,128)(2,1)S(1)}, bf16[32,4096]{1,0:T(8,128)(2,1)S(1)}, u32[]{:S(2)}, u32[]{:S(2)}) collective-permute-start(bf16[32,4096]{1,0:T(8,128)(2,1)S(1)} %reshape.21.refs_0_), channel_id=1, source_target_pairs={{0,64},{64,128},{128,192},{192,0},{1,65},{65,129},{129,193},{193,1... | collective-permute-start | bytes 786440 | tf_op jit(solution)/shard_map/ppermute | solution.py:18
  23.4 3.0 %collective-permute-start.2 = (bf16[32,4096]{1,0:T(8,128)(2,1)S(1)}, bf16[32,4096]{1,0:T(8,128)(2,1)S(1)}, u32[]{:S(2)}, u32[]{:S(2)}) collective-permute-start(bf16[32,4096]{1,0:T(8,128)(2,1)S(1)} %reshape.21.refs_0_), channel_id=1, source_target_pairs={{0,32},{32,0},{1,33},{33,1},{2,34},{34,2},{3,35},{35,3},{4,36},{36... | collective-permute-start | bytes 786440 | tf_op jit(solution)/shard_map/ppermute | solution.py:18
  26.4 1.3 %collective-permute-done.refs_1_ = bf16[32,4096]{1,0:T(8,128)(2,1)S(1)} collective-permute-done((bf16[32,4096]{1,0:T(8,128)(2,1)S(1)}, bf16[32,4096]{1,0:T(8,128)(2,1)S(1)}, u32[]{:S(2)}, u32[]{:S(2)}) %collective-permute-start) | collective-permute-done | bytes 262176 | tf_op jit(solution)/shard_map/ppermute | solution.py:18
  27.8 1.7 %collective-permute-start.9 = (bf16[16,4096]{1,0:T(8,128)(2,1)S(1)}, bf16[16,4096]{1,0:T(8,128)(2,1)S(1)}, u32[]{:S(2)}, u32[]{:S(2)}) collective-permute-start(bf16[16,4096]{1,0:T(8,128)(2,1)S(1)} %slice.32), channel_id=1, source_target_pairs={{0,64},{64,128},{128,192},{192,0},{1,65},{65,129},{129,193},{193,1... | collective-permute-start | bytes 393224 | tf_op jit(solution)/shard_map/ppermute | solution.py:18
  30.0 1.2 %collective-permute-done.2.refs_3_ = bf16[32,4096]{1,0:T(8,128)(2,1)S(1)} collective-permute-done((bf16[32,4096]{1,0:T(8,128)(2,1)S(1)}, bf16[32,4096]{1,0:T(8,128)(2,1)S(1)}, u32[]{:S(2)}, u32[]{:S(2)}) %collective-permute-start.2) | collective-permute-done | bytes 262176 | tf_op jit(solution)/shard_map/ppermute | solution.py:18
  31.3 1.7 %collective-permute-start.10 = (bf16[16,4096]{1,0:T(8,128)(2,1)S(1)}, bf16[16,4096]{1,0:T(8,128)(2,1)S(1)}, u32[]{:S(2)}, u32[]{:S(2)}) collective-permute-start(bf16[16,4096]{1,0:T(8,128)(2,1)S(1)} %slice.33), channel_id=1, source_target_pairs={{0,192},{64,0},{128,64},{192,128},{1,193},{65,1},{129,65},{193,129... | collective-permute-start | bytes 393224 | tf_op jit(solution)/shard_map/ppermute | solution.py:18
  32.9 2.8 %collective-permute-start.12 = (bf16[32,4096]{1,0:T(8,128)(2,1)S(1)}, bf16[32,4096]{1,0:T(8,128)(2,1)S(1)}, u32[]{:S(2)}, u32[]{:S(2)}) collective-permute-start(bf16[32,4096]{1,0:T(8,128)(2,1)S(1)} %collective-permute-done.2.refs_3_), channel_id=1, source_target_pairs={{0,192},{64,0},{128,64},{192,128},{1,193},{65,1},{129,65},{193,129... | collective-permute-start | bytes 786440 | tf_op jit(solution)/shard_map/ppermute | solution.py:18
  35.7 1.9 %collective-permute-done.10 = bf16[16,4096]{1,0:T(8,128)(2,1)S(1)} collective-permute-done((bf16[16,4096]{1,0:T(8,128)(2,1)S(1)}, bf16[16,4096]{1,0:T(8,128)(2,1)S(1)}, u32[]{:S(2)}, u32[]{:S(2)}) %collective-permute-start.10) | collective-permute-done | bytes 131104 | tf_op jit(solution)/shard_map/ppermute | solution.py:18
  37.6 1.6 %collective-permute-start.11 = (bf16[32,4096]{1,0:T(8,128)(2,1)S(1)}, bf16[32,4096]{1,0:T(8,128)(2,1)S(1)}, u32[]{:S(2)}, u32[]{:S(2)}) collective-permute-start(bf16[32,4096]{1,0:T(8,128)(2,1)S(1)} %collective-permute-done.2.refs_3_), channel_id=1, source_target_pairs={{0,64},{64,128},{128,192},{192,0},{1,65},{65,129},{129,193},{193,1... | collective-permute-start | bytes 786440 | tf_op jit(solution)/shard_map/ppermute | solution.py:18
  39.2 2.3 %collective-permute-done.12.refs_2_ = bf16[32,4096]{1,0:T(8,128)(2,1)S(1)} collective-permute-done((bf16[32,4096]{1,0:T(8,128)(2,1)S(1)}, bf16[32,4096]{1,0:T(8,128)(2,1)S(1)}, u32[]{:S(2)}, u32[]{:S(2)}) %collective-permute-start.12) | collective-permute-done | bytes 262176 | tf_op jit(solution)/shard_map/ppermute | solution.py:18
  41.6 3.0 %collective-permute-start.13 = (bf16[32,4096]{1,0:T(8,128)(2,1)S(1)}, bf16[32,4096]{1,0:T(8,128)(2,1)S(1)}, u32[]{:S(2)}, u32[]{:S(2)}) collective-permute-start(bf16[32,4096]{1,0:T(8,128)(2,1)S(1)} %constant_dynamic-update-slice_fusion.refs_0_), channel_id=1, source_target_pairs={{0,32},{32,0},{1,33},{33,1},{2,34},{34,2},{3,35},{35,3},{4,36},{36... | collective-permute-start | bytes 786440 | tf_op jit(solution)/shard_map/ppermute | solution.py:18
  44.6 5.1 %collective-permute-done.13.refs_3_ = bf16[32,4096]{1,0:T(8,128)(2,1)S(1)} collective-permute-done((bf16[32,4096]{1,0:T(8,128)(2,1)S(1)}, bf16[32,4096]{1,0:T(8,128)(2,1)S(1)}, u32[]{:S(2)}, u32[]{:S(2)}) %collective-permute-start.13) | collective-permute-done | bytes 262176 | tf_op jit(solution)/shard_map/ppermute | solution.py:18
  51.7 1.6 %collective-permute-start.14 = (bf16[128,512]{1,0:T(8,128)(2,1)S(1)}, bf16[128,512]{1,0:T(8,128)(2,1)S(1)}, u32[]{:S(2)}, u32[]{:S(2)}) collective-permute-start(bf16[128,512]{1,0:T(8,128)(2,1)S(1)} %convert_element_type.103), channel_id=1, source_target_pairs={{0,1},{1,0},{2,3},{3,2},{4,5},{5,4},{6,7},{7,6},{8,9},{9,8},{10,11... | collective-permute-start | bytes 393224 | tf_op jit(solution)/shard_map/ppermute | solution.py:18
  54.6 3.5 %collective-permute-done.14.came = bf16[128,512]{1,0:T(8,128)(2,1)S(1)} collective-permute-done((bf16[128,512]{1,0:T(8,128)(2,1)S(1)}, bf16[128,512]{1,0:T(8,128)(2,1)S(1)}, u32[]{:S(2)}, u32[]{:S(2)}) %collective-permute-start.14) | collective-permute-done | bytes 131104 | tf_op jit(solution)/shard_map/ppermute | solution.py:18
  58.9 3.1 %collective-permute-start.15 = (bf16[32,4096]{1,0:T(8,128)(2,1)S(1)}, bf16[32,4096]{1,0:T(8,128)(2,1)S(1)}, u32[]{:S(2)}, u32[]{:S(2)}) collective-permute-start(bf16[32,4096]{1,0:T(8,128)(2,1)S(1)} %get-tuple-element.17), channel_id=1, source_target_pairs={{0,32},{32,0},{1,33},{33,1},{2,34},{34,2},{3,35},{35,3},{4,36},{36... | collective-permute-start | bytes 786440 | tf_op jit(solution)/shard_map/ppermute | solution.py:18
  62.0 1.7 %collective-permute-start.20 = (bf16[32,4096]{1,0:T(8,128)(2,1)S(1)}, bf16[32,4096]{1,0:T(8,128)(2,1)S(1)}, u32[]{:S(2)}, u32[]{:S(2)}) collective-permute-start(bf16[32,4096]{1,0:T(8,128)(2,1)S(1)} %get-tuple-element.19), channel_id=1, source_target_pairs={{0,192},{64,0},{128,64},{192,128},{1,193},{65,1},{129,65},{193,129... | collective-permute-start | bytes 786440 | tf_op jit(solution)/shard_map/ppermute | solution.py:18
  64.9 2.6 %collective-permute-start.8 = (bf16[16,4096]{1,0:T(8,128)(2,1)S(1)}, bf16[16,4096]{1,0:T(8,128)(2,1)S(1)}, u32[]{:S(2)}, u32[]{:S(2)}) collective-permute-start(bf16[16,4096]{1,0:T(8,128)(2,1)S(1)} %slice.25), channel_id=1, source_target_pairs={{0,192},{64,0},{128,64},{192,128},{1,193},{65,1},{129,65},{193,129... | collective-permute-start | bytes 393224 | tf_op jit(solution)/shard_map/ppermute | solution.py:18
  68.2 2.7 %collective-permute-start.16 = (bf16[16,4096]{1,0:T(8,128)(2,1)S(1)}, bf16[16,4096]{1,0:T(8,128)(2,1)S(1)}, u32[]{:S(2)}, u32[]{:S(2)}) collective-permute-start(bf16[16,4096]{1,0:T(8,128)(2,1)S(1)} %get-tuple-element.21), channel_id=1, source_target_pairs={{0,192},{64,0},{128,64},{192,128},{1,193},{65,1},{129,65},{193,129... | collective-permute-start | bytes 393224 | tf_op jit(solution)/shard_map/ppermute | solution.py:18
  72.4 2.1 %collective-permute-done.16 = bf16[16,4096]{1,0:T(8,128)(2,1)S(1)} collective-permute-done((bf16[16,4096]{1,0:T(8,128)(2,1)S(1)}, bf16[16,4096]{1,0:T(8,128)(2,1)S(1)}, u32[]{:S(2)}, u32[]{:S(2)}) %collective-permute-start.16) | collective-permute-done | bytes 131104 | tf_op jit(solution)/shard_map/ppermute | solution.py:18
  74.6 2.9 %collective-permute-start.17 = (bf16[16,4096]{1,0:T(8,128)(2,1)S(1)}, bf16[16,4096]{1,0:T(8,128)(2,1)S(1)}, u32[]{:S(2)}, u32[]{:S(2)}) collective-permute-start(bf16[16,4096]{1,0:T(8,128)(2,1)S(1)} %add_convert_fusion.4), channel_id=1, source_target_pairs={{0,192},{64,0},{128,64},{192,128},{1,193},{65,1},{129,65},{193,129... | collective-permute-start | bytes 393224 | tf_op jit(solution)/shard_map/ppermute | solution.py:18
  78.4 1.6 %collective-permute-done.17 = bf16[16,4096]{1,0:T(8,128)(2,1)S(1)} collective-permute-done((bf16[16,4096]{1,0:T(8,128)(2,1)S(1)}, bf16[16,4096]{1,0:T(8,128)(2,1)S(1)}, u32[]{:S(2)}, u32[]{:S(2)}) %collective-permute-start.17) | collective-permute-done | bytes 131104 | tf_op jit(solution)/shard_map/ppermute | solution.py:18
  80.0 4.3 %collective-permute-done.19 = bf16[16,4096]{1,0:T(8,128)(2,1)S(1)} collective-permute-done((bf16[16,4096]{1,0:T(8,128)(2,1)S(1)}, bf16[16,4096]{1,0:T(8,128)(2,1)S(1)}, u32[]{:S(2)}, u32[]{:S(2)}) %collective-permute-start.19) | collective-permute-done | bytes 131104 | tf_op jit(solution)/shard_map/ppermute | solution.py:18
  84.5 13.7 %all_to_all.11 = bf16[8,4,4096]{2,1,0:T(4,128)(2,1)S(1)} all-to-all(bf16[8,4,4096]{2,1,0:T(4,128)(2,1)S(1)} %reshape.22), channel_id=1, replica_groups=mesh['y'=4,'h'=2,'z'=8,'c'=2,'fsdp'=2] {'z'}, dimensions={0} | all-to-all | bytes 524288 | tf_op jit(solution)/shard_map/all_to_all | solution.py:146
  (53 shorter events, 11.4 us)
Async XLA Ops:
  0.9 48.8 %copy-start.1 = (bf16[4096,128]{1,0:T(8,128)(2,1)S(1)}, bf16[4096,128]{1,0:T(8,128)(2,1)}, u32[]{:S(2)}) copy-start(bf16[4096,128]{1,0:T(8,128)(2,1)} %refs_4_.3) | copy-start | bytes 3145732
  21.3 6.5 %collective-permute-start = (bf16[32,4096]{1,0:T(8,128)(2,1)S(1)}, bf16[32,4096]{1,0:T(8,128)(2,1)S(1)}, u32[]{:S(2)}, u32[]{:S(2)}) collective-permute-start(bf16[32,4096]{1,0:T(8,128)(2,1)S(1)} %reshape.21.refs_0_), channel_id=1, source_target_pairs={{0,64},{64,128},{128,192},{192,0},{1,65},{65,129},{129,193},{193,1... | collective-permute-start | bytes 786440 | tf_op jit(solution)/shard_map/ppermute | solution.py:18
  22.9 7.0 %collective-permute-start.1 = (bf16[32,4096]{1,0:T(8,128)(2,1)S(1)}, bf16[32,4096]{1,0:T(8,128)(2,1)S(1)}, u32[]{:S(2)}, u32[]{:S(2)}) collective-permute-start(bf16[32,4096]{1,0:T(8,128)(2,1)S(1)} %reshape.21.refs_0_), channel_id=1, source_target_pairs={{0,192},{64,0},{128,64},{192,128},{1,193},{65,1},{129,65},{193,129... | collective-permute-start | bytes 786440 | tf_op jit(solution)/shard_map/ppermute | solution.py:18
  23.4 7.9 %collective-permute-start.2 = (bf16[32,4096]{1,0:T(8,128)(2,1)S(1)}, bf16[32,4096]{1,0:T(8,128)(2,1)S(1)}, u32[]{:S(2)}, u32[]{:S(2)}) collective-permute-start(bf16[32,4096]{1,0:T(8,128)(2,1)S(1)} %reshape.21.refs_0_), channel_id=1, source_target_pairs={{0,32},{32,0},{1,33},{33,1},{2,34},{34,2},{3,35},{35,3},{4,36},{36... | collective-permute-start | bytes 786440 | tf_op jit(solution)/shard_map/ppermute | solution.py:18
  27.8 5.2 %collective-permute-start.9 = (bf16[16,4096]{1,0:T(8,128)(2,1)S(1)}, bf16[16,4096]{1,0:T(8,128)(2,1)S(1)}, u32[]{:S(2)}, u32[]{:S(2)}) collective-permute-start(bf16[16,4096]{1,0:T(8,128)(2,1)S(1)} %slice.32), channel_id=1, source_target_pairs={{0,64},{64,128},{128,192},{192,0},{1,65},{65,129},{129,193},{193,1... | collective-permute-start | bytes 393224 | tf_op jit(solution)/shard_map/ppermute | solution.py:18
  29.4 15.2 %collective-permute-start.3 = (bf16[4096,128]{1,0:T(8,128)(2,1)}, bf16[4096,128]{1,0:T(8,128)(2,1)S(1)}, u32[]{:S(2)}, u32[]{:S(2)}) collective-permute-start(bf16[4096,128]{1,0:T(8,128)(2,1)} %refs_4_.3), channel_id=1, source_target_pairs={{0,2},{2,0},{1,3},{3,1},{4,6},{6,4},{5,7},{7,5},{8,10},{10,8},{9,1... | collective-permute-start | bytes 3145736 | tf_op jit(solution)/shard_map/ppermute | solution.py:18
  29.4 15.2 %collective-permute-start.4 = (bf16[4096,128]{1,0:T(8,128)(2,1)}, bf16[4096,128]{1,0:T(8,128)(2,1)S(1)}, u32[]{:S(2)}, u32[]{:S(2)}) collective-permute-start(bf16[4096,128]{1,0:T(8,128)(2,1)} %refs_6_.3), channel_id=1, source_target_pairs={{0,2},{2,0},{1,3},{3,1},{4,6},{6,4},{5,7},{7,5},{8,10},{10,8},{9,1... | collective-permute-start | bytes 3145736 | tf_op jit(solution)/shard_map/ppermute | solution.py:18
  29.9 24.7 %collective-permute-start.6 = (bf16[4096,128]{1,0:T(8,128)(2,1)S(1)}, bf16[4096,128]{1,0:T(8,128)(2,1)S(1)}, u32[]{:S(2)}, u32[]{:S(2)}) collective-permute-start(bf16[4096,128]{1,0:T(8,128)(2,1)S(1)} %copy-done), channel_id=1, source_target_pairs={{0,2},{2,0},{1,3},{3,1},{4,6},{6,4},{5,7},{7,5},{8,10},{10,8},{9,1... | collective-permute-start | bytes 3145736 | tf_op jit(solution)/shard_map/ppermute | solution.py:18
  31.3 6.4 %collective-permute-start.10 = (bf16[16,4096]{1,0:T(8,128)(2,1)S(1)}, bf16[16,4096]{1,0:T(8,128)(2,1)S(1)}, u32[]{:S(2)}, u32[]{:S(2)}) collective-permute-start(bf16[16,4096]{1,0:T(8,128)(2,1)S(1)} %slice.33), channel_id=1, source_target_pairs={{0,192},{64,0},{128,64},{192,128},{1,193},{65,1},{129,65},{193,129... | collective-permute-start | bytes 393224 | tf_op jit(solution)/shard_map/ppermute | solution.py:18
  32.9 8.6 %collective-permute-start.12 = (bf16[32,4096]{1,0:T(8,128)(2,1)S(1)}, bf16[32,4096]{1,0:T(8,128)(2,1)S(1)}, u32[]{:S(2)}, u32[]{:S(2)}) collective-permute-start(bf16[32,4096]{1,0:T(8,128)(2,1)S(1)} %collective-permute-done.2.refs_3_), channel_id=1, source_target_pairs={{0,192},{64,0},{128,64},{192,128},{1,193},{65,1},{129,65},{193,129... | collective-permute-start | bytes 786440 | tf_op jit(solution)/shard_map/ppermute | solution.py:18
  37.6 7.0 %collective-permute-start.11 = (bf16[32,4096]{1,0:T(8,128)(2,1)S(1)}, bf16[32,4096]{1,0:T(8,128)(2,1)S(1)}, u32[]{:S(2)}, u32[]{:S(2)}) collective-permute-start(bf16[32,4096]{1,0:T(8,128)(2,1)S(1)} %collective-permute-done.2.refs_3_), channel_id=1, source_target_pairs={{0,64},{64,128},{128,192},{192,0},{1,65},{65,129},{129,193},{193,1... | collective-permute-start | bytes 786440 | tf_op jit(solution)/shard_map/ppermute | solution.py:18
  41.6 8.1 %collective-permute-start.13 = (bf16[32,4096]{1,0:T(8,128)(2,1)S(1)}, bf16[32,4096]{1,0:T(8,128)(2,1)S(1)}, u32[]{:S(2)}, u32[]{:S(2)}) collective-permute-start(bf16[32,4096]{1,0:T(8,128)(2,1)S(1)} %constant_dynamic-update-slice_fusion.refs_0_), channel_id=1, source_target_pairs={{0,32},{32,0},{1,33},{33,1},{2,34},{34,2},{3,35},{35,3},{4,36},{36... | collective-permute-start | bytes 786440 | tf_op jit(solution)/shard_map/ppermute | solution.py:18
  51.7 6.5 %collective-permute-start.14 = (bf16[128,512]{1,0:T(8,128)(2,1)S(1)}, bf16[128,512]{1,0:T(8,128)(2,1)S(1)}, u32[]{:S(2)}, u32[]{:S(2)}) collective-permute-start(bf16[128,512]{1,0:T(8,128)(2,1)S(1)} %convert_element_type.103), channel_id=1, source_target_pairs={{0,1},{1,0},{2,3},{3,2},{4,5},{5,4},{6,7},{7,6},{8,9},{9,8},{10,11... | collective-permute-start | bytes 393224 | tf_op jit(solution)/shard_map/ppermute | solution.py:18
  54.0 10.1 %collective-permute-start.5 = (f32[128,512]{1,0:T(8,128)S(1)}, f32[128,512]{1,0:T(8,128)S(1)}, u32[]{:S(2)}, u32[]{:S(2)}) collective-permute-start(f32[128,512]{1,0:T(8,128)S(1)} %shard_map.46.parts), channel_id=1, source_target_pairs={{0,1},{1,0},{2,3},{3,2},{4,5},{5,4},{6,7},{7,6},{8,9},{9,8},{10,11... | collective-permute-start | bytes 786440 | tf_op jit(solution)/shard_map/ppermute | solution.py:18
  58.9 9.2 %collective-permute-start.15 = (bf16[32,4096]{1,0:T(8,128)(2,1)S(1)}, bf16[32,4096]{1,0:T(8,128)(2,1)S(1)}, u32[]{:S(2)}, u32[]{:S(2)}) collective-permute-start(bf16[32,4096]{1,0:T(8,128)(2,1)S(1)} %get-tuple-element.17), channel_id=1, source_target_pairs={{0,32},{32,0},{1,33},{33,1},{2,34},{34,2},{3,35},{35,3},{4,36},{36... | collective-permute-start | bytes 786440 | tf_op jit(solution)/shard_map/ppermute | solution.py:18
  62.0 8.9 %collective-permute-start.20 = (bf16[32,4096]{1,0:T(8,128)(2,1)S(1)}, bf16[32,4096]{1,0:T(8,128)(2,1)S(1)}, u32[]{:S(2)}, u32[]{:S(2)}) collective-permute-start(bf16[32,4096]{1,0:T(8,128)(2,1)S(1)} %get-tuple-element.19), channel_id=1, source_target_pairs={{0,192},{64,0},{128,64},{192,128},{1,193},{65,1},{129,65},{193,129... | collective-permute-start | bytes 786440 | tf_op jit(solution)/shard_map/ppermute | solution.py:18
  63.8 8.4 %collective-permute-start.21 = (bf16[32,4096]{1,0:T(8,128)(2,1)S(1)}, bf16[32,4096]{1,0:T(8,128)(2,1)S(1)}, u32[]{:S(2)}, u32[]{:S(2)}) collective-permute-start(bf16[32,4096]{1,0:T(8,128)(2,1)S(1)} %get-tuple-element.20), channel_id=1, source_target_pairs={{0,64},{64,128},{128,192},{192,0},{1,65},{65,129},{129,193},{193,1... | collective-permute-start | bytes 786440 | tf_op jit(solution)/shard_map/ppermute | solution.py:18
  64.9 13.5 %collective-permute-start.8 = (bf16[16,4096]{1,0:T(8,128)(2,1)S(1)}, bf16[16,4096]{1,0:T(8,128)(2,1)S(1)}, u32[]{:S(2)}, u32[]{:S(2)}) collective-permute-start(bf16[16,4096]{1,0:T(8,128)(2,1)S(1)} %slice.25), channel_id=1, source_target_pairs={{0,192},{64,0},{128,64},{192,128},{1,193},{65,1},{129,65},{193,129... | collective-permute-start | bytes 393224 | tf_op jit(solution)/shard_map/ppermute | solution.py:18
  67.5 10.9 %collective-permute-start.7 = (bf16[16,4096]{1,0:T(8,128)(2,1)S(1)}, bf16[16,4096]{1,0:T(8,128)(2,1)S(1)}, u32[]{:S(2)}, u32[]{:S(2)}) collective-permute-start(bf16[16,4096]{1,0:T(8,128)(2,1)S(1)} %slice.24), channel_id=1, source_target_pairs={{0,64},{64,128},{128,192},{192,0},{1,65},{65,129},{129,193},{193,1... | collective-permute-start | bytes 393224 | tf_op jit(solution)/shard_map/ppermute | solution.py:18
  68.2 6.3 %collective-permute-start.16 = (bf16[16,4096]{1,0:T(8,128)(2,1)S(1)}, bf16[16,4096]{1,0:T(8,128)(2,1)S(1)}, u32[]{:S(2)}, u32[]{:S(2)}) collective-permute-start(bf16[16,4096]{1,0:T(8,128)(2,1)S(1)} %get-tuple-element.21), channel_id=1, source_target_pairs={{0,192},{64,0},{128,64},{192,128},{1,193},{65,1},{129,65},{193,129... | collective-permute-start | bytes 393224 | tf_op jit(solution)/shard_map/ppermute | solution.py:18
  70.9 6.8 %collective-permute-start.18 = (bf16[16,4096]{1,0:T(8,128)(2,1)S(1)}, bf16[16,4096]{1,0:T(8,128)(2,1)S(1)}, u32[]{:S(2)}, u32[]{:S(2)}) collective-permute-start(bf16[16,4096]{1,0:T(8,128)(2,1)S(1)} %get-tuple-element.22), channel_id=1, source_target_pairs={{0,64},{64,128},{128,192},{192,0},{1,65},{65,129},{129,193},{193,1... | collective-permute-start | bytes 393224 | tf_op jit(solution)/shard_map/ppermute | solution.py:18
  72.3 12.0 %collective-permute-start.22 = (bf16[32,4096]{1,0:T(8,128)(2,1)S(1)}, bf16[32,4096]{1,0:T(8,128)(2,1)S(1)}, u32[]{:S(2)}, u32[]{:S(2)}) collective-permute-start(bf16[32,4096]{1,0:T(8,128)(2,1)S(1)} %add_convert_fusion.1), channel_id=1, source_target_pairs={{0,32},{32,0},{1,33},{33,1},{2,34},{34,2},{3,35},{35,3},{4,36},{36... | collective-permute-start | bytes 786440 | tf_op jit(solution)/shard_map/ppermute | solution.py:18
  74.6 5.4 %collective-permute-start.17 = (bf16[16,4096]{1,0:T(8,128)(2,1)S(1)}, bf16[16,4096]{1,0:T(8,128)(2,1)S(1)}, u32[]{:S(2)}, u32[]{:S(2)}) collective-permute-start(bf16[16,4096]{1,0:T(8,128)(2,1)S(1)} %add_convert_fusion.4), channel_id=1, source_target_pairs={{0,192},{64,0},{128,64},{192,128},{1,193},{65,1},{129,65},{193,129... | collective-permute-start | bytes 393224 | tf_op jit(solution)/shard_map/ppermute | solution.py:18
  77.7 6.5 %collective-permute-start.19 = (bf16[16,4096]{1,0:T(8,128)(2,1)S(1)}, bf16[16,4096]{1,0:T(8,128)(2,1)S(1)}, u32[]{:S(2)}, u32[]{:S(2)}) collective-permute-start(bf16[16,4096]{1,0:T(8,128)(2,1)S(1)} %add_convert_fusion.3), channel_id=1, source_target_pairs={{0,64},{64,128},{128,192},{192,0},{1,65},{65,129},{129,193},{193,1... | collective-permute-start | bytes 393224 | tf_op jit(solution)/shard_map/ppermute | solution.py:18
  (3 other events, 33.5 us)

commit v3 on v2

--- a/solution.py
+++ b/solution.py
@@ -32,7 +32,7 @@
     b_other = moved(other, "y", 1)
     a_other = moved(other, "y", 3)
     far_other = moved(far, "h", 1)
-    return (own, before, after, other), (far, b_other, a_other, far_other)
+    return (own, before, after), (other, far, b_other, a_other, far_other)
 
 
 def plus(first, *others):
@@ -62,12 +62,13 @@
     )(*args)
 
 
-def parts_of(blocks, gates, ups):
+def parts_of(blocks, gates, ups, kinds):
     depth, half = gates[0].shape
     rows = sum(b.shape[0] for b in blocks)
 
     def kernel(*refs):
-        *block_refs, g0, g1, u0, u1, out = refs
+        block_refs, weights = refs[: len(blocks)], refs[len(blocks) :]
+        g0, g1, u0, u1, *outs = weights
         for pair, at in (((g0, g1), 0), ((u0, u1), 2 * half)):
             total = jnp.zeros((rows, 2 * half), F32)
             for k in range(0, depth, STEP):
@@ -76,14 +77,15 @@
                 cut = (pl.ds(k, STEP), slice(None))
                 right = jnp.concatenate([w[cut] for w in pair], axis=1)
                 total += jnp.dot(left, right, preferred_element_type=F32)
-            out[:, at : at + 2 * half] = total
+            for out in outs:
+                out[:, at : at + 2 * half] = total.astype(out.dtype)
 
-    outs = [jax.ShapeDtypeStruct((rows, 4 * half), F32)]
+    outs = [jax.ShapeDtypeStruct((rows, 4 * half), kind) for kind in kinds]
     flops = 8 * rows * depth * half
-    return on_core(kernel, outs, flops, *blocks, *gates, *ups)[0]
+    return on_core(kernel, outs, flops, *blocks, *gates, *ups)
 
 
-def projected(parts, came, downs, sizes):
+def projected(parts, came, downs, pieces):
     width, half = downs[0].shape
 
     def kernel(parts, came, d0, d1, *outs):
@@ -91,40 +93,40 @@
         gate, up = values[:, : 2 * half], values[:, 2 * half :]
         hidden = (gate / (1 + jnp.exp(-gate)) * up).astype(BF16)
         for n in range(0, width, STEP):
-            cut = (pl.ds(n, STEP), slice(None))
+            cut = slice(n, n + STEP)
             right = jnp.concatenate([d0[cut], d1[cut]], axis=1)
             out = lax.dot_general(
                 hidden, right, (((1,), (1,)), ((), ())), preferred_element_type=F32
             ).astype(BF16)
             at = 0
-            for size, ref in zip(sizes, outs):
-                ref[:, n : n + STEP] = out[at : at + size]
-                at += size
+            for rows, ref in zip(pieces, outs):
+                ref[:, cut] = out[at : at + rows]
+                at += rows
 
-    outs = [jax.ShapeDtypeStruct((size, width), BF16) for size in sizes]
-    flops = 4 * sum(sizes) * width * half
+    outs = [jax.ShapeDtypeStruct((rows, width), BF16) for rows in pieces]
+    flops = 4 * parts.shape[0] * width * half
     return on_core(kernel, outs, flops, parts, came, *downs)
 
 
 def summed_in_plane(near, away):
-    own, before, after, other = near
-    far, b_other, a_other, far_other = away
+    own, before_top, before_bottom, after_top, after_bottom = near
+    other, far, b_other, a_other, far_other = away
     far = plus(far, moved(far_other, "h", 1))
-    from_after_o = moved(b_other, "y", 3)
-    from_before_o = moved(a_other, "y", 1)
+    from_after = moved(b_other, "y", 3)
+    from_before = moved(a_other, "y", 1)
     top, bottom = halves(far)
     top = moved(top, "y", 3)
     bottom = moved(bottom, "y", 1)
-    before_top, before_bottom = halves(before)
-    after_top, after_bottom = halves(after)
     early_top = moved(after_top, "y", 1)
     early_bottom = moved(before_bottom, "y", 3)
-    from_other = moved(plus(other, from_after_o, from_before_o), "h", 1)
+    from_other = moved(plus(other, from_after, from_before), "h", 1)
     late_top = moved(plus(before_top, top), "y", 3)
     late_bottom = moved(plus(after_bottom, bottom), "y", 1)
-    early = jnp.concatenate([early_top, early_bottom], axis=0)
-    late = jnp.concatenate([late_top, late_bottom], axis=0)
-    return plus(own, early, late, from_other)
+    own_top, own_bottom = halves(own)
+    other_top, other_bottom = halves(from_other)
+    top = plus(own_top, early_top, late_top, other_top)
+    bottom = plus(own_bottom, early_bottom, late_bottom, other_bottom)
+    return jnp.concatenate([top, bottom], axis=0)
 
 
 def on_device(tokens, gate_weight, up_weight, down_weight):
@@ -134,13 +136,14 @@
     downs = down_weight, moved(down_weight, "c", 1)
     own = shared(tokens, "z").reshape(-1, width)
     near, away = gathered_in_plane(own)
-    near = parts_of(near, gates, ups)
-    away = parts_of(away, gates, ups)
+    (near,) = parts_of(near, gates, ups, (F32,))
     near_in = moved(near, "fsdp", 1)
-    away_in = moved(away.astype(BF16), "fsdp", 1)
-    sizes = (own.shape[0],) * 4
-    away = projected(away, away_in, downs, sizes)
-    near = projected(near, near_in, downs, sizes)
+    away, sent = parts_of(away, gates, ups, (F32, BF16))
+    away_in = moved(sent, "fsdp", 1)
+    n = own.shape[0]
+    half = n // 2
+    near = projected(near, near_in, downs, (n, half, half, half, half))
+    away = projected(away, away_in, downs, (n,) * 5)
     mine = summed_in_plane(near, away)
     pieces = mine.reshape(-1, count, width)
     arrived = lax.all_to_all(pieces, "z", 0, 0, tiled=True)

time: 101 us -> 110 us (1.089)
  the two profiles are of different devices: /device:TPU:8 before, /device:TPU:2 now
where the time goes in v3:
time: 110 us; the launch traced here: 109 us
  waiting for transfers between devices  39.5 us (36%)
  blocking collectives  37 us (34%)
  starting transfers between devices  27.3 us (25%)
  Pallas kernels  3.23 us (3%)
  local copies, waits for them, and re-layouts  1.16 us (1%)
    ppermute x23, waiting for transfers between devices, moved(): return lax.ppermute(value, axis, [(i, (i + step) % n) for i in range(n)])  39.5 us
    ppermute x23, starting transfers between devices, moved(): return lax.ppermute(value, axis, [(i, (i + step) % n) for i in range(n)])  27.3 us
    all_to_all x1, blocking collectives, shared(): return lax.all_to_all(copies, axis, 0, 0, tiled=True)  20.3 us
    all_to_all x1, blocking collectives, on_device(): arrived = lax.all_to_all(pieces, 'z', 0, 0, tiled=True)  16.7 us
    pallas_call x4, Pallas kernels, on_core(): pl.pallas_call(kernel, out_shape=outs, in_specs=[vmem] * len(args), out_s...  3.23 us
  transfers between devices with their start and end apart: 23, of which 14 were waited for; matrix products, arithmetic and copies ran while one was open for 0% of the time, Pallas kernels for 2%

profile of v3, /device:TPU:2, one launch (start us, length us, event | category | flops | bytes accessed | tf_op | source)
XLA Modules:
  0.0 109.3 jit_solution(16427164570929126064)
XLA Ops:
  0.9 20.3 %all_to_all.10 = bf16[8,4,4096]{2,1,0:T(4,128)(2,1)S(1)} all-to-all(bf16[8,4,4096]{2,1,0:T(4,128)(2,1)S(1)} %broadcast_in_dim.3), channel_id=1, replica_groups=mesh['y'=4,'h'=2,'z'=8,'c'=2,'fsdp'=2] {'z'}, dimensions={0} | all-to-all | bytes 524288 | tf_op jit(solution)/shard_map/all_to_all | solution.py:23
  21.3 1.7 %collective-permute-start = (bf16[32,4096]{1,0:T(8,128)(2,1)S(1)}, bf16[32,4096]{1,0:T(8,128)(2,1)S(1)}, u32[]{:S(2)}, u32[]{:S(2)}) collective-permute-start(bf16[32,4096]{1,0:T(8,128)(2,1)S(1)} %reshape.21.refs_0_), channel_id=1, source_target_pairs={{0,64},{64,128},{128,192},{192,0},{1,65},{65,129},{129,193},{193,1... | collective-permute-start | bytes 786440 | tf_op jit(solution)/shard_map/ppermute | solution.py:18
  22.9 1.7 %collective-permute-start.1 = (bf16[32,4096]{1,0:T(8,128)(2,1)S(1)}, bf16[32,4096]{1,0:T(8,128)(2,1)S(1)}, u32[]{:S(2)}, u32[]{:S(2)}) collective-permute-start(bf16[32,4096]{1,0:T(8,128)(2,1)S(1)} %reshape.21.refs_0_), channel_id=1, source_target_pairs={{0,192},{64,0},{128,64},{192,128},{1,193},{65,1},{129,65},{193,129... | collective-permute-start | bytes 786440 | tf_op jit(solution)/shard_map/ppermute | solution.py:18
  24.6 2.1 %collective-permute-start.7 = (bf16[32,4096]{1,0:T(8,128)(2,1)S(1)}, bf16[32,4096]{1,0:T(8,128)(2,1)S(1)}, u32[]{:S(2)}, u32[]{:S(2)}) collective-permute-start(bf16[32,4096]{1,0:T(8,128)(2,1)S(1)} %reshape.21.refs_0_), channel_id=1, source_target_pairs={{0,32},{32,0},{1,33},{33,1},{2,34},{34,2},{3,35},{35,3},{4,36},{36... | collective-permute-start | bytes 786440 | tf_op jit(solution)/shard_map/ppermute | solution.py:18
  26.7 2.3 %collective-permute-done.refs_1_ = bf16[32,4096]{1,0:T(8,128)(2,1)S(1)} collective-permute-done((bf16[32,4096]{1,0:T(8,128)(2,1)S(1)}, bf16[32,4096]{1,0:T(8,128)(2,1)S(1)}, u32[]{:S(2)}, u32[]{:S(2)}) %collective-permute-start) | collective-permute-done | bytes 262176 | tf_op jit(solution)/shard_map/ppermute | solution.py:18
  29.9 2.5 %collective-permute-done.7.refs_0_ = bf16[32,4096]{1,0:T(8,128)(2,1)S(1)} collective-permute-done((bf16[32,4096]{1,0:T(8,128)(2,1)S(1)}, bf16[32,4096]{1,0:T(8,128)(2,1)S(1)}, u32[]{:S(2)}, u32[]{:S(2)}) %collective-permute-start.7) | collective-permute-done | bytes 262176 | tf_op jit(solution)/shard_map/ppermute | solution.py:18
  32.5 1.8 %collective-permute-start.9 = (bf16[16,4096]{1,0:T(8,128)(2,1)S(1)}, bf16[16,4096]{1,0:T(8,128)(2,1)S(1)}, u32[]{:S(2)}, u32[]{:S(2)}) collective-permute-start(bf16[16,4096]{1,0:T(8,128)(2,1)S(1)} %slice.33), channel_id=1, source_target_pairs={{0,192},{64,0},{128,64},{192,128},{1,193},{65,1},{129,65},{193,129... | collective-permute-start | bytes 393224 | tf_op jit(solution)/shard_map/ppermute | solution.py:18
  35.8 3.0 %collective-permute-done.9 = bf16[16,4096]{1,0:T(8,128)(2,1)S(1)} collective-permute-done((bf16[16,4096]{1,0:T(8,128)(2,1)S(1)}, bf16[16,4096]{1,0:T(8,128)(2,1)S(1)}, u32[]{:S(2)}, u32[]{:S(2)}) %collective-permute-start.9) | collective-permute-done | bytes 131104 | tf_op jit(solution)/shard_map/ppermute | solution.py:18
  39.2 3.6 %collective-permute-done.11.refs_3_ = bf16[32,4096]{1,0:T(8,128)(2,1)S(1)} collective-permute-done((bf16[32,4096]{1,0:T(8,128)(2,1)S(1)}, bf16[32,4096]{1,0:T(8,128)(2,1)S(1)}, u32[]{:S(2)}, u32[]{:S(2)}) %collective-permute-start.11) | collective-permute-done | bytes 262176 | tf_op jit(solution)/shard_map/ppermute | solution.py:18
  42.8 2.1 %collective-permute-start.12 = (bf16[32,4096]{1,0:T(8,128)(2,1)S(1)}, bf16[32,4096]{1,0:T(8,128)(2,1)S(1)}, u32[]{:S(2)}, u32[]{:S(2)}) collective-permute-start(bf16[32,4096]{1,0:T(8,128)(2,1)S(1)} %constant_dynamic-update-slice_fusion.refs_1_), channel_id=1, source_target_pairs={{0,32},{32,0},{1,33},{33,1},{2,34},{34,2},{3,35},{35,3},{4,36},{36... | collective-permute-start | bytes 786440 | tf_op jit(solution)/shard_map/ppermute | solution.py:18
  44.9 1.5 %collective-permute-done.10.refs_2_ = bf16[32,4096]{1,0:T(8,128)(2,1)S(1)} collective-permute-done((bf16[32,4096]{1,0:T(8,128)(2,1)S(1)}, bf16[32,4096]{1,0:T(8,128)(2,1)S(1)}, u32[]{:S(2)}, u32[]{:S(2)}) %collective-permute-start.10) | collective-permute-done | bytes 262176 | tf_op jit(solution)/shard_map/ppermute | solution.py:18
  46.4 4.6 %collective-permute-done.12.refs_4_ = bf16[32,4096]{1,0:T(8,128)(2,1)S(1)} collective-permute-done((bf16[32,4096]{1,0:T(8,128)(2,1)S(1)}, bf16[32,4096]{1,0:T(8,128)(2,1)S(1)}, u32[]{:S(2)}, u32[]{:S(2)}) %collective-permute-start.12) | collective-permute-done | bytes 262176 | tf_op jit(solution)/shard_map/ppermute | solution.py:18
  52.5 4.8 %collective-permute-done.13.came = bf16[160,512]{1,0:T(8,128)(2,1)S(1)} collective-permute-done((bf16[160,512]{1,0:T(8,128)(2,1)S(1)}, bf16[160,512]{1,0:T(8,128)(2,1)S(1)}, u32[]{:S(2)}, u32[]{:S(2)}) %collective-permute-start.13) | collective-permute-done | bytes 163872 | tf_op jit(solution)/shard_map/ppermute | solution.py:18
  58.1 2.9 %collective-permute-start.14 = (bf16[32,4096]{1,0:T(8,128)(2,1)S(1)}, bf16[32,4096]{1,0:T(8,128)(2,1)S(1)}, u32[]{:S(2)}, u32[]{:S(2)}) collective-permute-start(bf16[32,4096]{1,0:T(8,128)(2,1)S(1)} %get-tuple-element.23), channel_id=1, source_target_pairs={{0,32},{32,0},{1,33},{33,1},{2,34},{34,2},{3,35},{35,3},{4,36},{36... | collective-permute-start | bytes 786440 | tf_op jit(solution)/shard_map/ppermute | solution.py:18
  62.6 6.0 %collective-permute-done.4.came = f32[96,512]{1,0:T(8,128)S(1)} collective-permute-done((f32[96,512]{1,0:T(8,128)S(1)}, f32[96,512]{1,0:T(8,128)S(1)}, u32[]{:S(2)}, u32[]{:S(2)}) %collective-permute-start.4) | collective-permute-done | bytes 196640 | tf_op jit(solution)/shard_map/ppermute | solution.py:18
  69.9 3.0 %collective-permute-start.20 = (bf16[16,4096]{1,0:T(8,128)(2,1)S(1)}, bf16[16,4096]{1,0:T(8,128)(2,1)S(1)}, u32[]{:S(2)}, u32[]{:S(2)}) collective-permute-start(bf16[16,4096]{1,0:T(8,128)(2,1)S(1)} %get-tuple-element.27), channel_id=1, source_target_pairs={{0,192},{64,0},{128,64},{192,128},{1,193},{65,1},{129,65},{193,129... | collective-permute-start | bytes 393224 | tf_op jit(solution)/shard_map/ppermute | solution.py:18
  72.8 1.4 %collective-permute-start.17 = (bf16[32,4096]{1,0:T(8,128)(2,1)S(1)}, bf16[32,4096]{1,0:T(8,128)(2,1)S(1)}, u32[]{:S(2)}, u32[]{:S(2)}) collective-permute-start(bf16[32,4096]{1,0:T(8,128)(2,1)S(1)} %get-tuple-element.25), channel_id=1, source_target_pairs={{0,192},{64,0},{128,64},{192,128},{1,193},{65,1},{129,65},{193,129... | collective-permute-start | bytes 786440 | tf_op jit(solution)/shard_map/ppermute | solution.py:18
  75.0 2.7 %collective-permute-start.15 = (bf16[16,4096]{1,0:T(8,128)(2,1)S(1)}, bf16[16,4096]{1,0:T(8,128)(2,1)S(1)}, u32[]{:S(2)}, u32[]{:S(2)}) collective-permute-start(bf16[16,4096]{1,0:T(8,128)(2,1)S(1)} %get-tuple-element.31), channel_id=1, source_target_pairs={{0,192},{64,0},{128,64},{192,128},{1,193},{65,1},{129,65},{193,129... | collective-permute-start | bytes 393224 | tf_op jit(solution)/shard_map/ppermute | solution.py:18
  77.7 1.5 %collective-permute-done.17 = bf16[32,4096]{1,0:T(8,128)(2,1)S(1)} collective-permute-done((bf16[32,4096]{1,0:T(8,128)(2,1)S(1)}, bf16[32,4096]{1,0:T(8,128)(2,1)S(1)}, u32[]{:S(2)}, u32[]{:S(2)}) %collective-permute-start.17) | collective-permute-done | bytes 262176 | tf_op jit(solution)/shard_map/ppermute | solution.py:18
  79.6 2.3 %collective-permute-done.18 = bf16[32,4096]{1,0:T(8,128)(2,1)S(1)} collective-permute-done((bf16[32,4096]{1,0:T(8,128)(2,1)S(1)}, bf16[32,4096]{1,0:T(8,128)(2,1)S(1)}, u32[]{:S(2)}, u32[]{:S(2)}) %collective-permute-start.18) | collective-permute-done | bytes 262176 | tf_op jit(solution)/shard_map/ppermute | solution.py:18
  82.9 2.1 %collective-permute-start.16 = (bf16[16,4096]{1,0:T(8,128)(2,1)S(1)}, bf16[16,4096]{1,0:T(8,128)(2,1)S(1)}, u32[]{:S(2)}, u32[]{:S(2)}) collective-permute-start(bf16[16,4096]{1,0:T(8,128)(2,1)S(1)} %add_convert_fusion.5), channel_id=1, source_target_pairs={{0,192},{64,0},{128,64},{192,128},{1,193},{65,1},{129,65},{193,129... | collective-permute-start | bytes 393224 | tf_op jit(solution)/shard_map/ppermute | solution.py:18
  85.5 2.4 %collective-permute-done.16 = bf16[16,4096]{1,0:T(8,128)(2,1)S(1)} collective-permute-done((bf16[16,4096]{1,0:T(8,128)(2,1)S(1)}, bf16[16,4096]{1,0:T(8,128)(2,1)S(1)}, u32[]{:S(2)}, u32[]{:S(2)}) %collective-permute-start.16) | collective-permute-done | bytes 131104 | tf_op jit(solution)/shard_map/ppermute | solution.py:18
  88.0 3.7 %collective-permute-done.22 = bf16[16,4096]{1,0:T(8,128)(2,1)S(1)} collective-permute-done((bf16[16,4096]{1,0:T(8,128)(2,1)S(1)}, bf16[16,4096]{1,0:T(8,128)(2,1)S(1)}, u32[]{:S(2)}, u32[]{:S(2)}) %collective-permute-start.22) | collective-permute-done | bytes 131104 | tf_op jit(solution)/shard_map/ppermute | solution.py:18
  92.0 16.7 %all_to_all.11 = bf16[8,4,4096]{2,1,0:T(4,128)(2,1)S(1)} all-to-all(bf16[8,4,4096]{2,1,0:T(4,128)(2,1)S(1)} %reshape.22), channel_id=1, replica_groups=mesh['y'=4,'h'=2,'z'=8,'c'=2,'fsdp'=2] {'z'}, dimensions={0} | all-to-all | bytes 524288 | tf_op jit(solution)/shard_map/all_to_all | solution.py:149
  (49 shorter events, 12.5 us)
Async XLA Ops:
  0.9 50.1 %copy-start.1 = (bf16[4096,128]{1,0:T(8,128)(2,1)S(1)}, bf16[4096,128]{1,0:T(8,128)(2,1)}, u32[]{:S(2)}) copy-start(bf16[4096,128]{1,0:T(8,128)(2,1)} %refs_7_.1) | copy-start | bytes 3145732
  21.3 7.7 %collective-permute-start = (bf16[32,4096]{1,0:T(8,128)(2,1)S(1)}, bf16[32,4096]{1,0:T(8,128)(2,1)S(1)}, u32[]{:S(2)}, u32[]{:S(2)}) collective-permute-start(bf16[32,4096]{1,0:T(8,128)(2,1)S(1)} %reshape.21.refs_0_), channel_id=1, source_target_pairs={{0,64},{64,128},{128,192},{192,0},{1,65},{65,129},{129,193},{193,1... | collective-permute-start | bytes 786440 | tf_op jit(solution)/shard_map/ppermute | solution.py:18
  22.9 7.0 %collective-permute-start.1 = (bf16[32,4096]{1,0:T(8,128)(2,1)S(1)}, bf16[32,4096]{1,0:T(8,128)(2,1)S(1)}, u32[]{:S(2)}, u32[]{:S(2)}) collective-permute-start(bf16[32,4096]{1,0:T(8,128)(2,1)S(1)} %reshape.21.refs_0_), channel_id=1, source_target_pairs={{0,192},{64,0},{128,64},{192,128},{1,193},{65,1},{129,65},{193,129... | collective-permute-start | bytes 786440 | tf_op jit(solution)/shard_map/ppermute | solution.py:18
  24.6 7.9 %collective-permute-start.7 = (bf16[32,4096]{1,0:T(8,128)(2,1)S(1)}, bf16[32,4096]{1,0:T(8,128)(2,1)S(1)}, u32[]{:S(2)}, u32[]{:S(2)}) collective-permute-start(bf16[32,4096]{1,0:T(8,128)(2,1)S(1)} %reshape.21.refs_0_), channel_id=1, source_target_pairs={{0,32},{32,0},{1,33},{33,1},{2,34},{34,2},{3,35},{35,3},{4,36},{36... | collective-permute-start | bytes 786440 | tf_op jit(solution)/shard_map/ppermute | solution.py:18
  29.0 6.3 %collective-permute-start.8 = (bf16[16,4096]{1,0:T(8,128)(2,1)S(1)}, bf16[16,4096]{1,0:T(8,128)(2,1)S(1)}, u32[]{:S(2)}, u32[]{:S(2)}) collective-permute-start(bf16[16,4096]{1,0:T(8,128)(2,1)S(1)} %slice.32), channel_id=1, source_target_pairs={{0,64},{64,128},{128,192},{192,0},{1,65},{65,129},{129,193},{193,1... | collective-permute-start | bytes 393224 | tf_op jit(solution)/shard_map/ppermute | solution.py:18
  29.4 17.0 %collective-permute-start.2 = (bf16[4096,128]{1,0:T(8,128)(2,1)S(1)}, bf16[4096,128]{1,0:T(8,128)(2,1)S(1)}, u32[]{:S(2)}, u32[]{:S(2)}) collective-permute-start(bf16[4096,128]{1,0:T(8,128)(2,1)S(1)} %copy-done), channel_id=1, source_target_pairs={{0,2},{2,0},{1,3},{3,1},{4,6},{6,4},{5,7},{7,5},{8,10},{10,8},{9,1... | collective-permute-start | bytes 3145736 | tf_op jit(solution)/shard_map/ppermute | solution.py:18
  29.4 17.0 %collective-permute-start.3 = (bf16[4096,128]{1,0:T(8,128)(2,1)}, bf16[4096,128]{1,0:T(8,128)(2,1)S(1)}, u32[]{:S(2)}, u32[]{:S(2)}) collective-permute-start(bf16[4096,128]{1,0:T(8,128)(2,1)} %refs_7_.1), channel_id=1, source_target_pairs={{0,2},{2,0},{1,3},{3,1},{4,6},{6,4},{5,7},{7,5},{8,10},{10,8},{9,1... | collective-permute-start | bytes 3145736 | tf_op jit(solution)/shard_map/ppermute | solution.py:18
  29.9 22.5 %collective-permute-start.5 = (bf16[4096,128]{1,0:T(8,128)(2,1)}, bf16[4096,128]{1,0:T(8,128)(2,1)S(1)}, u32[]{:S(2)}, u32[]{:S(2)}) collective-permute-start(bf16[4096,128]{1,0:T(8,128)(2,1)} %d0.3), channel_id=1, source_target_pairs={{0,2},{2,0},{1,3},{3,1},{4,6},{6,4},{5,7},{7,5},{8,10},{10,8},{9,1... | collective-permute-start | bytes 3145736 | tf_op jit(solution)/shard_map/ppermute | solution.py:18
  32.5 6.4 %collective-permute-start.9 = (bf16[16,4096]{1,0:T(8,128)(2,1)S(1)}, bf16[16,4096]{1,0:T(8,128)(2,1)S(1)}, u32[]{:S(2)}, u32[]{:S(2)}) collective-permute-start(bf16[16,4096]{1,0:T(8,128)(2,1)S(1)} %slice.33), channel_id=1, source_target_pairs={{0,192},{64,0},{128,64},{192,128},{1,193},{65,1},{129,65},{193,129... | collective-permute-start | bytes 393224 | tf_op jit(solution)/shard_map/ppermute | solution.py:18
  35.3 7.5 %collective-permute-start.11 = (bf16[32,4096]{1,0:T(8,128)(2,1)S(1)}, bf16[32,4096]{1,0:T(8,128)(2,1)S(1)}, u32[]{:S(2)}, u32[]{:S(2)}) collective-permute-start(bf16[32,4096]{1,0:T(8,128)(2,1)S(1)} %collective-permute-done.7.refs_0_), channel_id=1, source_target_pairs={{0,192},{64,0},{128,64},{192,128},{1,193},{65,1},{129,65},{193,129... | collective-permute-start | bytes 786440 | tf_op jit(solution)/shard_map/ppermute | solution.py:18
  38.8 7.6 %collective-permute-start.10 = (bf16[32,4096]{1,0:T(8,128)(2,1)S(1)}, bf16[32,4096]{1,0:T(8,128)(2,1)S(1)}, u32[]{:S(2)}, u32[]{:S(2)}) collective-permute-start(bf16[32,4096]{1,0:T(8,128)(2,1)S(1)} %collective-permute-done.7.refs_0_), channel_id=1, source_target_pairs={{0,64},{64,128},{128,192},{192,0},{1,65},{65,129},{129,193},{193,1... | collective-permute-start | bytes 786440 | tf_op jit(solution)/shard_map/ppermute | solution.py:18
  42.8 8.2 %collective-permute-start.12 = (bf16[32,4096]{1,0:T(8,128)(2,1)S(1)}, bf16[32,4096]{1,0:T(8,128)(2,1)S(1)}, u32[]{:S(2)}, u32[]{:S(2)}) collective-permute-start(bf16[32,4096]{1,0:T(8,128)(2,1)S(1)} %constant_dynamic-update-slice_fusion.refs_1_), channel_id=1, source_target_pairs={{0,32},{32,0},{1,33},{33,1},{2,34},{34,2},{3,35},{35,3},{4,36},{36... | collective-permute-start | bytes 786440 | tf_op jit(solution)/shard_map/ppermute | solution.py:18
  51.8 5.4 %collective-permute-start.13 = (bf16[160,512]{1,0:T(8,128)(2,1)S(1)}, bf16[160,512]{1,0:T(8,128)(2,1)S(1)}, u32[]{:S(2)}, u32[]{:S(2)}) collective-permute-start(bf16[160,512]{1,0:T(8,128)(2,1)S(1)} %get-tuple-element.21), channel_id=1, source_target_pairs={{0,1},{1,0},{2,3},{3,2},{4,5},{5,4},{6,7},{7,6},{8,9},{9,8},{10,11... | collective-permute-start | bytes 491528 | tf_op jit(solution)/shard_map/ppermute | solution.py:18
  58.1 16.8 %collective-permute-start.14 = (bf16[32,4096]{1,0:T(8,128)(2,1)S(1)}, bf16[32,4096]{1,0:T(8,128)(2,1)S(1)}, u32[]{:S(2)}, u32[]{:S(2)}) collective-permute-start(bf16[32,4096]{1,0:T(8,128)(2,1)S(1)} %get-tuple-element.23), channel_id=1, source_target_pairs={{0,32},{32,0},{1,33},{33,1},{2,34},{34,2},{3,35},{35,3},{4,36},{36... | collective-permute-start | bytes 786440 | tf_op jit(solution)/shard_map/ppermute | solution.py:18
  61.8 6.8 %collective-permute-start.4 = (f32[96,512]{1,0:T(8,128)S(1)}, f32[96,512]{1,0:T(8,128)S(1)}, u32[]{:S(2)}, u32[]{:S(2)}) collective-permute-start(f32[96,512]{1,0:T(8,128)S(1)} %shard_map.46.parts), channel_id=1, source_target_pairs={{0,1},{1,0},{2,3},{3,2},{4,5},{5,4},{6,7},{7,6},{8,9},{9,8},{10,11... | collective-permute-start | bytes 589832 | tf_op jit(solution)/shard_map/ppermute | solution.py:18
  69.3 16.2 %collective-permute-start.6 = (bf16[16,4096]{1,0:T(8,128)(2,1)S(1)}, bf16[16,4096]{1,0:T(8,128)(2,1)S(1)}, u32[]{:S(2)}, u32[]{:S(2)}) collective-permute-start(bf16[16,4096]{1,0:T(8,128)(2,1)S(1)} %get-tuple-element.18), channel_id=1, source_target_pairs={{0,64},{64,128},{128,192},{192,0},{1,65},{65,129},{129,193},{193,1... | collective-permute-start | bytes 393224 | tf_op jit(solution)/shard_map/ppermute | solution.py:18
  69.9 15.7 %collective-permute-start.20 = (bf16[16,4096]{1,0:T(8,128)(2,1)S(1)}, bf16[16,4096]{1,0:T(8,128)(2,1)S(1)}, u32[]{:S(2)}, u32[]{:S(2)}) collective-permute-start(bf16[16,4096]{1,0:T(8,128)(2,1)S(1)} %get-tuple-element.27), channel_id=1, source_target_pairs={{0,192},{64,0},{128,64},{192,128},{1,193},{65,1},{129,65},{193,129... | collective-permute-start | bytes 393224 | tf_op jit(solution)/shard_map/ppermute | solution.py:18
  72.8 6.4 %collective-permute-start.17 = (bf16[32,4096]{1,0:T(8,128)(2,1)S(1)}, bf16[32,4096]{1,0:T(8,128)(2,1)S(1)}, u32[]{:S(2)}, u32[]{:S(2)}) collective-permute-start(bf16[32,4096]{1,0:T(8,128)(2,1)S(1)} %get-tuple-element.25), channel_id=1, source_target_pairs={{0,192},{64,0},{128,64},{192,128},{1,193},{65,1},{129,65},{193,129... | collective-permute-start | bytes 786440 | tf_op jit(solution)/shard_map/ppermute | solution.py:18
  74.3 7.6 %collective-permute-start.18 = (bf16[32,4096]{1,0:T(8,128)(2,1)S(1)}, bf16[32,4096]{1,0:T(8,128)(2,1)S(1)}, u32[]{:S(2)}, u32[]{:S(2)}) collective-permute-start(bf16[32,4096]{1,0:T(8,128)(2,1)S(1)} %get-tuple-element.26), channel_id=1, source_target_pairs={{0,64},{64,128},{128,192},{192,0},{1,65},{65,129},{129,193},{193,1... | collective-permute-start | bytes 786440 | tf_op jit(solution)/shard_map/ppermute | solution.py:18
  75.0 7.9 %collective-permute-start.15 = (bf16[16,4096]{1,0:T(8,128)(2,1)S(1)}, bf16[16,4096]{1,0:T(8,128)(2,1)S(1)}, u32[]{:S(2)}, u32[]{:S(2)}) collective-permute-start(bf16[16,4096]{1,0:T(8,128)(2,1)S(1)} %get-tuple-element.31), channel_id=1, source_target_pairs={{0,192},{64,0},{128,64},{192,128},{1,193},{65,1},{129,65},{193,129... | collective-permute-start | bytes 393224 | tf_op jit(solution)/shard_map/ppermute | solution.py:18
  79.2 6.2 %collective-permute-start.21 = (bf16[16,4096]{1,0:T(8,128)(2,1)S(1)}, bf16[16,4096]{1,0:T(8,128)(2,1)S(1)}, u32[]{:S(2)}, u32[]{:S(2)}) collective-permute-start(bf16[16,4096]{1,0:T(8,128)(2,1)S(1)} %get-tuple-element.32), channel_id=1, source_target_pairs={{0,64},{64,128},{128,192},{192,0},{1,65},{65,129},{129,193},{193,1... | collective-permute-start | bytes 393224 | tf_op jit(solution)/shard_map/ppermute | solution.py:18
  82.0 9.7 %collective-permute-start.19 = (bf16[32,4096]{1,0:T(8,128)(2,1)S(1)}, bf16[32,4096]{1,0:T(8,128)(2,1)S(1)}, u32[]{:S(2)}, u32[]{:S(2)}) collective-permute-start(bf16[32,4096]{1,0:T(8,128)(2,1)S(1)} %add_convert_fusion), channel_id=1, source_target_pairs={{0,32},{32,0},{1,33},{33,1},{2,34},{34,2},{3,35},{35,3},{4,36},{36... | collective-permute-start | bytes 786440 | tf_op jit(solution)/shard_map/ppermute | solution.py:18
  82.9 5.0 %collective-permute-start.16 = (bf16[16,4096]{1,0:T(8,128)(2,1)S(1)}, bf16[16,4096]{1,0:T(8,128)(2,1)S(1)}, u32[]{:S(2)}, u32[]{:S(2)}) collective-permute-start(bf16[16,4096]{1,0:T(8,128)(2,1)S(1)} %add_convert_fusion.5), channel_id=1, source_target_pairs={{0,192},{64,0},{128,64},{192,128},{1,193},{65,1},{129,65},{193,129... | collective-permute-start | bytes 393224 | tf_op jit(solution)/shard_map/ppermute | solution.py:18
  85.4 6.3 %collective-permute-start.22 = (bf16[16,4096]{1,0:T(8,128)(2,1)S(1)}, bf16[16,4096]{1,0:T(8,128)(2,1)S(1)}, u32[]{:S(2)}, u32[]{:S(2)}) collective-permute-start(bf16[16,4096]{1,0:T(8,128)(2,1)S(1)} %add_convert_fusion.3), channel_id=1, source_target_pairs={{0,64},{64,128},{128,192},{192,0},{1,65},{65,129},{129,193},{193,1... | collective-permute-start | bytes 393224 | tf_op jit(solution)/shard_map/ppermute | solution.py:18
  (2 other events, 47.4 us)

commit v4 on v3

--- a/solution.py
+++ b/solution.py
@@ -24,15 +24,14 @@
 
 
 def gathered_in_plane(own):
+    far = moved(own, "y", 2)
+    other = moved(own, "h", 1)
     before = moved(own, "y", 1)
     after = moved(own, "y", 3)
-    other = moved(own, "h", 1)
-    far = [moved(halves(before)[0], "y", 1), moved(halves(after)[1], "y", 3)]
-    far = jnp.concatenate(far, axis=0)
     b_other = moved(other, "y", 1)
     a_other = moved(other, "y", 3)
     far_other = moved(far, "h", 1)
-    return (own, before, after), (other, far, b_other, a_other, far_other)
+    return (own, before, after), (other, far), (b_other, a_other, far_other)
 
 
 def plus(first, *others):
@@ -40,11 +39,6 @@
     for other in others:
         total = total + other.astype(F32)
     return total.astype(BF16)
-
-
-def halves(value):
-    half = value.shape[0] // 2
-    return value[:half], value[half:]
 
 
 def on_core(kernel, outs, flops, *args):
@@ -60,6 +54,22 @@
             flops=flops, transcendentals=0, bytes_accessed=moved_bytes
         ),
     )(*args)
+
+
+def held(value):
+    def kernel(source, out, sem):
+        copy = pltpu.make_async_copy(source, out, sem)
+        copy.start()
+        copy.wait()
+
+    return pl.pallas_call(
+        kernel,
+        out_shape=jax.ShapeDtypeStruct(value.shape, value.dtype),
+        in_specs=[pl.BlockSpec(memory_space=pl.ANY)],
+        out_specs=pl.BlockSpec(memory_space=pltpu.VMEM),
+        scratch_shapes=[pltpu.SemaphoreType.DMA],
+        compiler_params=pltpu.CompilerParams(vmem_limit_bytes=VMEM_LIMIT),
+    )(value)
 
 
 def parts_of(blocks, gates, ups, kinds):
@@ -108,43 +118,40 @@
     return on_core(kernel, outs, flops, parts, came, *downs)
 
 
-def summed_in_plane(near, away):
-    own, before_top, before_bottom, after_top, after_bottom = near
-    other, far, b_other, a_other, far_other = away
+def summed_in_plane(near, mid, away):
+    own, before, after = near
+    other, far = mid
+    b_other, a_other, far_other = away
     far = plus(far, moved(far_other, "h", 1))
     from_after = moved(b_other, "y", 3)
     from_before = moved(a_other, "y", 1)
-    top, bottom = halves(far)
-    top = moved(top, "y", 3)
-    bottom = moved(bottom, "y", 1)
-    early_top = moved(after_top, "y", 1)
-    early_bottom = moved(before_bottom, "y", 3)
-    from_other = moved(plus(other, from_after, from_before), "h", 1)
-    late_top = moved(plus(before_top, top), "y", 3)
-    late_bottom = moved(plus(after_bottom, bottom), "y", 1)
-    own_top, own_bottom = halves(own)
-    other_top, other_bottom = halves(from_other)
-    top = plus(own_top, early_top, late_top, other_top)
-    bottom = plus(own_bottom, early_bottom, late_bottom, other_bottom)
-    return jnp.concatenate([top, bottom], axis=0)
+    other = plus(other, from_after, from_before)
+    from_after = moved(before, "y", 3)
+    from_before = moved(after, "y", 1)
+    from_far = moved(far, "y", 2)
+    from_other = moved(other, "h", 1)
+    return plus(own, from_after, from_before, from_far, from_other)
 
 
 def on_device(tokens, gate_weight, up_weight, down_weight):
     count, width = tokens.shape
+    up_weight = held(up_weight)
     gates = gate_weight, moved(gate_weight, "c", 1)
     ups = up_weight, moved(up_weight, "c", 1)
     downs = down_weight, moved(down_weight, "c", 1)
     own = shared(tokens, "z").reshape(-1, width)
-    near, away = gathered_in_plane(own)
+    near, mid, away = gathered_in_plane(own)
     (near,) = parts_of(near, gates, ups, (F32,))
     near_in = moved(near, "fsdp", 1)
+    (mid,) = parts_of(mid, gates, ups, (F32,))
+    mid_in = moved(mid, "fsdp", 1)
     away, sent = parts_of(away, gates, ups, (F32, BF16))
     away_in = moved(sent, "fsdp", 1)
     n = own.shape[0]
-    half = n // 2
-    near = projected(near, near_in, downs, (n, half, half, half, half))
-    away = projected(away, away_in, downs, (n,) * 5)
-    mine = summed_in_plane(near, away)
+    near = projected(near, near_in, downs, (n,) * 3)
+    mid = projected(mid, mid_in, downs, (n, n))
+    away = projected(away, away_in, downs, (n,) * 3)
+    mine = summed_in_plane(near, mid, away)
     pieces = mine.reshape(-1, count, width)
     arrived = lax.all_to_all(pieces, "z", 0, 0, tiled=True)
     return plus(*arrived)

time: 110 us -> 104 us (0.945)
  the two profiles are of different devices: /device:TPU:2 before, /device:TPU:8 now
where the time goes in v4:
time: 104 us; the launch traced here: 103 us
  starting transfers between devices  41.3 us (40%)
  waiting for transfers between devices  29.4 us (28%)
  Pallas kernels  13.1 us (13%)
  blocking collectives  12.9 us (12%)
  local copies, waits for them, and re-layouts  4.91 us (5%)
    ppermute x20, starting transfers between devices, moved(): return lax.ppermute(value, axis, [(i, (i + step) % n) for i in range(n)])  32.8 us
    ppermute x20, waiting for transfers between devices, moved(): return lax.ppermute(value, axis, [(i, (i + step) % n) for i in range(n)])  20.3 us
    pallas_call x6, Pallas kernels, on_core(): pl.pallas_call(kernel, out_shape=outs, in_specs=[vmem] * len(args), out_s...  13 us
    all_to_all x1, blocking collectives, on_device(): arrived = lax.all_to_all(pieces, 'z', 0, 0, tiled=True)  12.9 us
    all_to_all x1, waiting for transfers between devices, shared(): return lax.all_to_all(copies, axis, 0, 0, tiled=True)  9.02 us
    all_to_all x1, starting transfers between devices, shared(): return lax.all_to_all(copies, axis, 0, 0, tiled=True)  8.47 us
    unnamed x4, local copies, waits for them, and re-layouts  2.26 us
  transfers between devices with their start and end apart: 21, of which 12 were waited for; matrix products, arithmetic and copies ran while one was open for 1% of the time, Pallas kernels for 13%

profile of v4, /device:TPU:8, one launch (start us, length us, event | category | flops | bytes accessed | tf_op | source)
XLA Modules:
  0.0 102.6 jit_solution(18337982346044194814)
XLA Ops:
  1.5 8.5 %all-to-all-start = ((bf16[8,4,4096]{2,1,0:T(4,128)(2,1)}), bf16[8,4,4096]{2,1,0:T(4,128)(2,1)}, u32[]{:S(2)}, u32[]{:S(2)}) async-start(bf16[8,4,4096]{2,1,0:T(4,128)(2,1)} %broadcast_in_dim.3), calls=%async_computation | async-start | bytes 524288 | tf_op jit(solution)/shard_map/all_to_all | solution.py:23
  13.0 9.0 %all-to-all-done = bf16[8,4,4096]{2,1,0:T(4,128)(2,1)} async-done(((bf16[8,4,4096]{2,1,0:T(4,128)(2,1)}), bf16[8,4,4096]{2,1,0:T(4,128)(2,1)}, u32[]{:S(2)}, u32[]{:S(2)}) %all-to-all-start) | async-done | bytes 262176 | tf_op jit(solution)/shard_map/all_to_all | solution.py:23
  23.0 2.4 %collective-permute-start.9 = (bf16[32,4096]{1,0:T(8,128)(2,1)S(1)}, bf16[32,4096]{1,0:T(8,128)(2,1)S(1)}, u32[]{:S(2)}, u32[]{:S(2)}) collective-permute-start(bf16[32,4096]{1,0:T(8,128)(2,1)S(1)} %reshape.21.refs_0_), channel_id=1, source_target_pairs={{0,128},{64,192},{128,0},{192,64},{1,129},{65,193},{129,1},{193,65... | collective-permute-start | bytes 786440 | tf_op jit(solution)/shard_map/ppermute | solution.py:18
  25.4 3.0 %collective-permute-start.8 = (bf16[32,4096]{1,0:T(8,128)(2,1)S(1)}, bf16[32,4096]{1,0:T(8,128)(2,1)S(1)}, u32[]{:S(2)}, u32[]{:S(2)}) collective-permute-start(bf16[32,4096]{1,0:T(8,128)(2,1)S(1)} %reshape.21.refs_0_), channel_id=1, source_target_pairs={{0,32},{32,0},{1,33},{33,1},{2,34},{34,2},{3,35},{35,3},{4,36},{36... | collective-permute-start | bytes 786440 | tf_op jit(solution)/shard_map/ppermute | solution.py:18
  28.4 2.6 %collective-permute-done.9.refs_1_ = bf16[32,4096]{1,0:T(8,128)(2,1)S(1)} collective-permute-done((bf16[32,4096]{1,0:T(8,128)(2,1)S(1)}, bf16[32,4096]{1,0:T(8,128)(2,1)S(1)}, u32[]{:S(2)}, u32[]{:S(2)}) %collective-permute-start.9) | collective-permute-done | bytes 262176 | tf_op jit(solution)/shard_map/ppermute | solution.py:18
  31.0 3.0 %collective-permute-start.13 = (bf16[32,4096]{1,0:T(8,128)(2,1)S(1)}, bf16[32,4096]{1,0:T(8,128)(2,1)S(1)}, u32[]{:S(2)}, u32[]{:S(2)}) collective-permute-start(bf16[32,4096]{1,0:T(8,128)(2,1)S(1)} %collective-permute-done.9.refs_1_), channel_id=1, source_target_pairs={{0,32},{32,0},{1,33},{33,1},{2,34},{34,2},{3,35},{35,3},{4,36},{36... | collective-permute-start | bytes 786440 | tf_op jit(solution)/shard_map/ppermute | solution.py:18
  34.1 2.2 %collective-permute-start.12 = (bf16[32,4096]{1,0:T(8,128)(2,1)S(1)}, bf16[32,4096]{1,0:T(8,128)(2,1)S(1)}, u32[]{:S(2)}, u32[]{:S(2)}) collective-permute-start(bf16[32,4096]{1,0:T(8,128)(2,1)S(1)} %collective-permute-done.8.refs_0_), channel_id=1, source_target_pairs={{0,192},{64,0},{128,64},{192,128},{1,193},{65,1},{129,65},{193,129... | collective-permute-start | bytes 786440 | tf_op jit(solution)/shard_map/ppermute | solution.py:18
  36.4 2.5 %collective-permute-done.13.refs_2_ = bf16[32,4096]{1,0:T(8,128)(2,1)S(1)} collective-permute-done((bf16[32,4096]{1,0:T(8,128)(2,1)S(1)}, bf16[32,4096]{1,0:T(8,128)(2,1)S(1)}, u32[]{:S(2)}, u32[]{:S(2)}) %collective-permute-start.13) | collective-permute-done | bytes 262176 | tf_op jit(solution)/shard_map/ppermute | solution.py:18
  41.9 2.5 %collective-permute-start.1 = (bf16[32,4096]{1,0:T(8,128)(2,1)S(1)}, bf16[32,4096]{1,0:T(8,128)(2,1)S(1)}, u32[]{:S(2)}, u32[]{:S(2)}) collective-permute-start(bf16[32,4096]{1,0:T(8,128)(2,1)S(1)} %reshape.21.refs_0_), channel_id=1, source_target_pairs={{0,192},{64,0},{128,64},{192,128},{1,193},{65,1},{129,65},{193,129... | collective-permute-start | bytes 786440 | tf_op jit(solution)/shard_map/ppermute | solution.py:18
  46.3 2.5 %collective-permute-start = (bf16[32,4096]{1,0:T(8,128)(2,1)S(1)}, bf16[32,4096]{1,0:T(8,128)(2,1)S(1)}, u32[]{:S(2)}, u32[]{:S(2)}) collective-permute-start(bf16[32,4096]{1,0:T(8,128)(2,1)S(1)} %reshape.21.refs_0_), channel_id=1, source_target_pairs={{0,64},{64,128},{128,192},{192,0},{1,65},{65,129},{129,193},{193,1... | collective-permute-start | bytes 786440 | tf_op jit(solution)/shard_map/ppermute | solution.py:18
  48.8 2.0 %shard_map.51 = (f32[96,512]{1,0:T(8,128)S(1)}, bf16[96,512]{1,0:T(8,128)(2,1)S(1)}) custom-call(bf16[32,4096]{1,0:T(8,128)(2,1)S(1)} %collective-permute-done.11.refs_0_, bf16[32,4096]{1,0:T(8,128)(2,1)S(1)} %collective-permute-done.12.refs_1_, bf16[32,4096]{1,0:T(8,128)(2,1)S(1)} %collective-permute-done.13.refs_2_, bf16[4096,128]{1,0:T(8,128)(2,1)S(1)} %copy-done, ...), custom_call_target="tpu_custom_call" | custom-call | flops 402653184 | bytes 5275648 | tf_op jit(solution)/shard_map/pallas_call | solution.py:47
  52.2 4.2 %collective-permute-done.14.came = bf16[96,512]{1,0:T(8,128)(2,1)S(1)} collective-permute-done((bf16[96,512]{1,0:T(8,128)(2,1)S(1)}, bf16[96,512]{1,0:T(8,128)(2,1)S(1)}, u32[]{:S(2)}, u32[]{:S(2)}) %collective-permute-start.14) | collective-permute-done | bytes 98336 | tf_op jit(solution)/shard_map/ppermute | solution.py:18
  56.4 2.3 %shard_map.52 = (bf16[32,4096]{1,0:T(8,128)(2,1)S(1)}, bf16[32,4096]{1,0:T(8,128)(2,1)S(1)}, bf16[32,4096]{1,0:T(8,128)(2,1)S(1)}) custom-call(f32[96,512]{1,0:T(8,128)S(1)} %get-tuple-element.19.parts, bf16[96,512]{1,0:T(8,128)(2,1)S(1)} %collective-permute-done.14.came, bf16[4096,128]{1,0:T(8,128)(2,1)} %d0.5, bf16[4096,128]{1,0:T(8,128)(2,1)} %collective-permute-done.5.d1), custom_call_target="tpu_custom_call" | custom-call | flops 201326592 | bytes 3178496 | tf_op jit(solution)/shard_map/pallas_call | solution.py:47
  58.7 3.1 %collective-permute-start.15 = (bf16[32,4096]{1,0:T(8,128)(2,1)S(1)}, bf16[32,4096]{1,0:T(8,128)(2,1)S(1)}, u32[]{:S(2)}, u32[]{:S(2)}) collective-permute-start(bf16[32,4096]{1,0:T(8,128)(2,1)S(1)} %get-tuple-element.21), channel_id=1, source_target_pairs={{0,32},{32,0},{1,33},{33,1},{2,34},{34,2},{3,35},{35,3},{4,36},{36... | collective-permute-start | bytes 786440 | tf_op jit(solution)/shard_map/ppermute | solution.py:18
  61.8 2.0 %shard_map.47.parts = f32[96,512]{1,0:T(8,128)S(1)} custom-call(bf16[32,4096]{1,0:T(8,128)(2,1)S(1)} %reshape.21.refs_0_, bf16[32,4096]{1,0:T(8,128)(2,1)S(1)} %collective-permute-done.refs_1_, bf16[32,4096]{1,0:T(8,128)(2,1)S(1)} %collective-permute-done.1.refs_2_, bf16[4096,128]{1,0:T(8,128)(2,1)S(1)} %copy-done, ...), custom_call_target="tpu_custom_call" | custom-call | flops 402653184 | bytes 5177344 | tf_op jit(solution)/shard_map/pallas_call | solution.py:47
  64.1 2.1 %shard_map.49.parts = f32[64,512]{1,0:T(8,128)S(1)} custom-call(bf16[32,4096]{1,0:T(8,128)(2,1)S(1)} %collective-permute-done.8.refs_0_, bf16[32,4096]{1,0:T(8,128)(2,1)S(1)} %collective-permute-done.9.refs_1_, bf16[4096,128]{1,0:T(8,128)(2,1)S(1)} %copy-done, bf16[4096,128]{1,0:T(8,128)(2,1)} %collective-permute-done.2.refs_4_.refs_3_, ...), custom_call_target="tpu_custom_call" | custom-call | flops 268435456 | bytes 4849664 | tf_op jit(solution)/shard_map/pallas_call | solution.py:47
  68.0 2.0 %collective-permute-start.18 = (bf16[32,4096]{1,0:T(8,128)(2,1)S(1)}, bf16[32,4096]{1,0:T(8,128)(2,1)S(1)}, u32[]{:S(2)}, u32[]{:S(2)}) collective-permute-start(bf16[32,4096]{1,0:T(8,128)(2,1)S(1)} %get-tuple-element.24), channel_id=1, source_target_pairs={{0,64},{64,128},{128,192},{192,0},{1,65},{65,129},{129,193},{193,1... | collective-permute-start | bytes 786440 | tf_op jit(solution)/shard_map/ppermute | solution.py:18
  71.2 2.3 %shard_map.50 = (bf16[32,4096]{1,0:T(8,128)(2,1)S(1)}, bf16[32,4096]{1,0:T(8,128)(2,1)S(1)}) custom-call(f32[64,512]{1,0:T(8,128)S(1)} %shard_map.49.parts, f32[64,512]{1,0:T(8,128)S(1)} %collective-permute-done.10.came, bf16[4096,128]{1,0:T(8,128)(2,1)} %d0.5, bf16[4096,128]{1,0:T(8,128)(2,1)} %collective-permute-done.5.d1), custom_call_target="tpu_custom_call" | custom-call | flops 134217728 | bytes 2883584 | tf_op jit(solution)/shard_map/pallas_call | solution.py:47
  73.5 2.3 %shard_map.48 = (bf16[32,4096]{1,0:T(8,128)(2,1)S(1)}, bf16[32,4096]{1,0:T(8,128)(2,1)S(1)}, bf16[32,4096]{1,0:T(8,128)(2,1)S(1)}) custom-call(f32[96,512]{1,0:T(8,128)S(1)} %shard_map.47.parts, f32[96,512]{1,0:T(8,128)S(1)} %collective-permute-done.4.came, bf16[4096,128]{1,0:T(8,128)(2,1)} %d0.5, bf16[4096,128]{1,0:T(8,128)(2,1)} %collective-permute-done.5.d1), custom_call_target="tpu_custom_call" | custom-call | flops 201326592 | bytes 3276800 | tf_op jit(solution)/shard_map/pallas_call | solution.py:47
  75.9 2.0 %collective-permute-start.7 = (bf16[32,4096]{1,0:T(8,128)(2,1)S(1)}, bf16[32,4096]{1,0:T(8,128)(2,1)S(1)}, u32[]{:S(2)}, u32[]{:S(2)}) collective-permute-start(bf16[32,4096]{1,0:T(8,128)(2,1)S(1)} %get-tuple-element.17), channel_id=1, source_target_pairs={{0,64},{64,128},{128,192},{192,0},{1,65},{65,129},{129,193},{193,1... | collective-permute-start | bytes 786440 | tf_op jit(solution)/shard_map/ppermute | solution.py:18
  78.0 2.6 %collective-permute-start.16 = (bf16[32,4096]{1,0:T(8,128)(2,1)S(1)}, bf16[32,4096]{1,0:T(8,128)(2,1)S(1)}, u32[]{:S(2)}, u32[]{:S(2)}) collective-permute-start(bf16[32,4096]{1,0:T(8,128)(2,1)S(1)} %add_convert_fusion.2), channel_id=1, source_target_pairs={{0,128},{64,192},{128,0},{192,64},{1,129},{65,193},{129,1},{193,65... | collective-permute-start | bytes 786440 | tf_op jit(solution)/shard_map/ppermute | solution.py:18
  83.3 2.7 %collective-permute-done.16 = bf16[32,4096]{1,0:T(8,128)(2,1)S(1)} collective-permute-done((bf16[32,4096]{1,0:T(8,128)(2,1)S(1)}, bf16[32,4096]{1,0:T(8,128)(2,1)S(1)}, u32[]{:S(2)}, u32[]{:S(2)}) %collective-permute-start.16) | collective-permute-done | bytes 262176 | tf_op jit(solution)/shard_map/ppermute | solution.py:18
  86.0 2.8 %collective-permute-done.19 = bf16[32,4096]{1,0:T(8,128)(2,1)S(1)} collective-permute-done((bf16[32,4096]{1,0:T(8,128)(2,1)S(1)}, bf16[32,4096]{1,0:T(8,128)(2,1)S(1)}, u32[]{:S(2)}, u32[]{:S(2)}) %collective-permute-start.19) | collective-permute-done | bytes 262176 | tf_op jit(solution)/shard_map/ppermute | solution.py:18
  89.0 12.9 %all_to_all.10 = bf16[8,4,4096]{2,1,0:T(4,128)(2,1)S(1)} all-to-all(bf16[8,4,4096]{2,1,0:T(4,128)(2,1)S(1)} %reshape.22), channel_id=1, replica_groups=mesh['y'=4,'h'=2,'z'=8,'c'=2,'fsdp'=2] {'z'}, dimensions={0} | all-to-all | bytes 524288 | tf_op jit(solution)/shard_map/all_to_all | solution.py:156
  (37 shorter events, 19.0 us)
Async XLA Ops:
  1.5 20.4 %all-to-all-start = ((bf16[8,4,4096]{2,1,0:T(4,128)(2,1)}), bf16[8,4,4096]{2,1,0:T(4,128)(2,1)}, u32[]{:S(2)}, u32[]{:S(2)}) async-start(bf16[8,4,4096]{2,1,0:T(4,128)(2,1)} %broadcast_in_dim.3), calls=%async_computation | async-start | bytes 524288 | tf_op jit(solution)/shard_map/all_to_all | solution.py:23
  10.0 1.2 %copy-start.1 = (bf16[4096,128]{1,0:T(8,128)(2,1)S(1)}, bf16[4096,128]{1,0:T(8,128)(2,1)}, u32[]{:S(2)}) copy-start(bf16[4096,128]{1,0:T(8,128)(2,1)} %source.1) | copy-start | bytes 3145732
  11.2 1.2 %copy-start = (bf16[4096,128]{1,0:T(8,128)(2,1)S(1)}, bf16[4096,128]{1,0:T(8,128)(2,1)}, u32[]{:S(2)}) copy-start(bf16[4096,128]{1,0:T(8,128)(2,1)} %refs_3_.3) | copy-start | bytes 3145732
  11.3 37.5 %collective-permute-start.3 = (bf16[4096,128]{1,0:T(8,128)(2,1)S(1)}, bf16[4096,128]{1,0:T(8,128)(2,1)S(1)}, u32[]{:S(2)}, u32[]{:S(2)}) collective-permute-start(bf16[4096,128]{1,0:T(8,128)(2,1)S(1)} %shard_map.46.refs_5_.refs_4_), channel_id=1, source_target_pairs={{0,2},{2,0},{1,3},{3,1},{4,6},{6,4},{5,7},{7,5},{8,10},{10,8},{9,1... | collective-permute-start | bytes 3145736 | tf_op jit(solution)/shard_map/ppermute | solution.py:18
  12.5 36.3 %collective-permute-start.2 = (bf16[4096,128]{1,0:T(8,128)(2,1)S(1)}, bf16[4096,128]{1,0:T(8,128)(2,1)}, u32[]{:S(2)}, u32[]{:S(2)}) collective-permute-start(bf16[4096,128]{1,0:T(8,128)(2,1)S(1)} %copy-done), channel_id=1, source_target_pairs={{0,2},{2,0},{1,3},{3,1},{4,6},{6,4},{5,7},{7,5},{8,10},{10,8},{9,1... | collective-permute-start | bytes 3145736 | tf_op jit(solution)/shard_map/ppermute | solution.py:18
  12.5 39.7 %collective-permute-start.5 = (bf16[4096,128]{1,0:T(8,128)(2,1)}, bf16[4096,128]{1,0:T(8,128)(2,1)}, u32[]{:S(2)}, u32[]{:S(2)}) collective-permute-start(bf16[4096,128]{1,0:T(8,128)(2,1)} %d0.5), channel_id=1, source_target_pairs={{0,2},{2,0},{1,3},{3,1},{4,6},{6,4},{5,7},{7,5},{8,10},{10,8},{9,1... | collective-permute-start | bytes 3145736 | tf_op jit(solution)/shard_map/ppermute | solution.py:18
  23.0 8.0 %collective-permute-start.9 = (bf16[32,4096]{1,0:T(8,128)(2,1)S(1)}, bf16[32,4096]{1,0:T(8,128)(2,1)S(1)}, u32[]{:S(2)}, u32[]{:S(2)}) collective-permute-start(bf16[32,4096]{1,0:T(8,128)(2,1)S(1)} %reshape.21.refs_0_), channel_id=1, source_target_pairs={{0,128},{64,192},{128,0},{192,64},{1,129},{65,193},{129,1},{193,65... | collective-permute-start | bytes 786440 | tf_op jit(solution)/shard_map/ppermute | solution.py:18
  25.4 8.7 %collective-permute-start.8 = (bf16[32,4096]{1,0:T(8,128)(2,1)S(1)}, bf16[32,4096]{1,0:T(8,128)(2,1)S(1)}, u32[]{:S(2)}, u32[]{:S(2)}) collective-permute-start(bf16[32,4096]{1,0:T(8,128)(2,1)S(1)} %reshape.21.refs_0_), channel_id=1, source_target_pairs={{0,32},{32,0},{1,33},{33,1},{2,34},{34,2},{3,35},{35,3},{4,36},{36... | collective-permute-start | bytes 786440 | tf_op jit(solution)/shard_map/ppermute | solution.py:18
  31.0 7.9 %collective-permute-start.13 = (bf16[32,4096]{1,0:T(8,128)(2,1)S(1)}, bf16[32,4096]{1,0:T(8,128)(2,1)S(1)}, u32[]{:S(2)}, u32[]{:S(2)}) collective-permute-start(bf16[32,4096]{1,0:T(8,128)(2,1)S(1)} %collective-permute-done.9.refs_1_), channel_id=1, source_target_pairs={{0,32},{32,0},{1,33},{33,1},{2,34},{34,2},{3,35},{35,3},{4,36},{36... | collective-permute-start | bytes 786440 | tf_op jit(solution)/shard_map/ppermute | solution.py:18
  34.1 7.8 %collective-permute-start.12 = (bf16[32,4096]{1,0:T(8,128)(2,1)S(1)}, bf16[32,4096]{1,0:T(8,128)(2,1)S(1)}, u32[]{:S(2)}, u32[]{:S(2)}) collective-permute-start(bf16[32,4096]{1,0:T(8,128)(2,1)S(1)} %collective-permute-done.8.refs_0_), channel_id=1, source_target_pairs={{0,192},{64,0},{128,64},{192,128},{1,193},{65,1},{129,65},{193,129... | collective-permute-start | bytes 786440 | tf_op jit(solution)/shard_map/ppermute | solution.py:18
  38.9 7.4 %collective-permute-start.11 = (bf16[32,4096]{1,0:T(8,128)(2,1)S(1)}, bf16[32,4096]{1,0:T(8,128)(2,1)S(1)}, u32[]{:S(2)}, u32[]{:S(2)}) collective-permute-start(bf16[32,4096]{1,0:T(8,128)(2,1)S(1)} %collective-permute-done.8.refs_0_), channel_id=1, source_target_pairs={{0,64},{64,128},{128,192},{192,0},{1,65},{65,129},{129,193},{193,1... | collective-permute-start | bytes 786440 | tf_op jit(solution)/shard_map/ppermute | solution.py:18
  41.9 19.8 %collective-permute-start.1 = (bf16[32,4096]{1,0:T(8,128)(2,1)S(1)}, bf16[32,4096]{1,0:T(8,128)(2,1)S(1)}, u32[]{:S(2)}, u32[]{:S(2)}) collective-permute-start(bf16[32,4096]{1,0:T(8,128)(2,1)S(1)} %reshape.21.refs_0_), channel_id=1, source_target_pairs={{0,192},{64,0},{128,64},{192,128},{1,193},{65,1},{129,65},{193,129... | collective-permute-start | bytes 786440 | tf_op jit(solution)/shard_map/ppermute | solution.py:18
  46.3 15.5 %collective-permute-start = (bf16[32,4096]{1,0:T(8,128)(2,1)S(1)}, bf16[32,4096]{1,0:T(8,128)(2,1)S(1)}, u32[]{:S(2)}, u32[]{:S(2)}) collective-permute-start(bf16[32,4096]{1,0:T(8,128)(2,1)S(1)} %reshape.21.refs_0_), channel_id=1, source_target_pairs={{0,64},{64,128},{128,192},{192,0},{1,65},{65,129},{129,193},{193,1... | collective-permute-start | bytes 786440 | tf_op jit(solution)/shard_map/ppermute | solution.py:18
  50.8 5.6 %collective-permute-start.14 = (bf16[96,512]{1,0:T(8,128)(2,1)S(1)}, bf16[96,512]{1,0:T(8,128)(2,1)S(1)}, u32[]{:S(2)}, u32[]{:S(2)}) collective-permute-start(bf16[96,512]{1,0:T(8,128)(2,1)S(1)} %get-tuple-element.20), channel_id=1, source_target_pairs={{0,1},{1,0},{2,3},{3,2},{4,5},{5,4},{6,7},{7,6},{8,9},{9,8},{10,11... | collective-permute-start | bytes 294920 | tf_op jit(solution)/shard_map/ppermute | solution.py:18
  58.7 19.3 %collective-permute-start.15 = (bf16[32,4096]{1,0:T(8,128)(2,1)S(1)}, bf16[32,4096]{1,0:T(8,128)(2,1)S(1)}, u32[]{:S(2)}, u32[]{:S(2)}) collective-permute-start(bf16[32,4096]{1,0:T(8,128)(2,1)S(1)} %get-tuple-element.21), channel_id=1, source_target_pairs={{0,32},{32,0},{1,33},{33,1},{2,34},{34,2},{3,35},{35,3},{4,36},{36... | collective-permute-start | bytes 786440 | tf_op jit(solution)/shard_map/ppermute | solution.py:18
  63.8 9.8 %collective-permute-start.4 = (f32[96,512]{1,0:T(8,128)S(1)}, f32[96,512]{1,0:T(8,128)S(1)}, u32[]{:S(2)}, u32[]{:S(2)}) collective-permute-start(f32[96,512]{1,0:T(8,128)S(1)} %shard_map.47.parts), channel_id=1, source_target_pairs={{0,1},{1,0},{2,3},{3,2},{4,5},{5,4},{6,7},{7,6},{8,9},{9,8},{10,11... | collective-permute-start | bytes 589832 | tf_op jit(solution)/shard_map/ppermute | solution.py:18
  66.2 5.1 %collective-permute-start.10 = (f32[64,512]{1,0:T(8,128)S(1)}, f32[64,512]{1,0:T(8,128)S(1)}, u32[]{:S(2)}, u32[]{:S(2)}) collective-permute-start(f32[64,512]{1,0:T(8,128)S(1)} %shard_map.49.parts), channel_id=1, source_target_pairs={{0,1},{1,0},{2,3},{3,2},{4,5},{5,4},{6,7},{7,6},{8,9},{9,8},{10,11... | collective-permute-start | bytes 393224 | tf_op jit(solution)/shard_map/ppermute | solution.py:18
  68.0 12.6 %collective-permute-start.17 = (bf16[32,4096]{1,0:T(8,128)(2,1)S(1)}, bf16[32,4096]{1,0:T(8,128)(2,1)S(1)}, u32[]{:S(2)}, u32[]{:S(2)}) collective-permute-start(bf16[32,4096]{1,0:T(8,128)(2,1)S(1)} %get-tuple-element.23), channel_id=1, source_target_pairs={{0,192},{64,0},{128,64},{192,128},{1,193},{65,1},{129,65},{193,129... | collective-permute-start | bytes 786440 | tf_op jit(solution)/shard_map/ppermute | solution.py:18
  68.0 12.6 %collective-permute-start.18 = (bf16[32,4096]{1,0:T(8,128)(2,1)S(1)}, bf16[32,4096]{1,0:T(8,128)(2,1)S(1)}, u32[]{:S(2)}, u32[]{:S(2)}) collective-permute-start(bf16[32,4096]{1,0:T(8,128)(2,1)S(1)} %get-tuple-element.24), channel_id=1, source_target_pairs={{0,64},{64,128},{128,192},{192,0},{1,65},{65,129},{129,193},{193,1... | collective-permute-start | bytes 786440 | tf_op jit(solution)/shard_map/ppermute | solution.py:18
  75.9 7.3 %collective-permute-start.6 = (bf16[32,4096]{1,0:T(8,128)(2,1)S(1)}, bf16[32,4096]{1,0:T(8,128)(2,1)S(1)}, u32[]{:S(2)}, u32[]{:S(2)}) collective-permute-start(bf16[32,4096]{1,0:T(8,128)(2,1)S(1)} %get-tuple-element.16), channel_id=1, source_target_pairs={{0,192},{64,0},{128,64},{192,128},{1,193},{65,1},{129,65},{193,129... | collective-permute-start | bytes 786440 | tf_op jit(solution)/shard_map/ppermute | solution.py:18
  75.9 7.3 %collective-permute-start.7 = (bf16[32,4096]{1,0:T(8,128)(2,1)S(1)}, bf16[32,4096]{1,0:T(8,128)(2,1)S(1)}, u32[]{:S(2)}, u32[]{:S(2)}) collective-permute-start(bf16[32,4096]{1,0:T(8,128)(2,1)S(1)} %get-tuple-element.17), channel_id=1, source_target_pairs={{0,64},{64,128},{128,192},{192,0},{1,65},{65,129},{129,193},{193,1... | collective-permute-start | bytes 786440 | tf_op jit(solution)/shard_map/ppermute | solution.py:18
  78.0 8.0 %collective-permute-start.16 = (bf16[32,4096]{1,0:T(8,128)(2,1)S(1)}, bf16[32,4096]{1,0:T(8,128)(2,1)S(1)}, u32[]{:S(2)}, u32[]{:S(2)}) collective-permute-start(bf16[32,4096]{1,0:T(8,128)(2,1)S(1)} %add_convert_fusion.2), channel_id=1, source_target_pairs={{0,128},{64,192},{128,0},{192,64},{1,129},{65,193},{129,1},{193,65... | collective-permute-start | bytes 786440 | tf_op jit(solution)/shard_map/ppermute | solution.py:18
  80.8 8.0 %collective-permute-start.19 = (bf16[32,4096]{1,0:T(8,128)(2,1)S(1)}, bf16[32,4096]{1,0:T(8,128)(2,1)S(1)}, u32[]{:S(2)}, u32[]{:S(2)}) collective-permute-start(bf16[32,4096]{1,0:T(8,128)(2,1)S(1)} %add_convert_fusion.1), channel_id=1, source_target_pairs={{0,32},{32,0},{1,33},{33,1},{2,34},{34,2},{3,35},{35,3},{4,36},{36... | collective-permute-start | bytes 786440 | tf_op jit(solution)/shard_map/ppermute | solution.py:18
